TPU v7x, 32 devices: a whole 2x2x4 slice. The times are simulated.
32 devices in a mesh: orb: 4 (over x, core), gx: 2 (over y), gyz: 4 (over z).
Axes of the slice: x: 2, y: 2, z: 4, core: 2. Of those that a mesh axis runs over, the one named last changes fastest.
Arguments:
- orbitals: float32 [2, 12, 32, 32, 128], P(None, 'orb', 'gx', 'gyz'), parts along dimension 1, may hold values from -12 to 12
- potential: float32 [32, 32, 128], P('gx', 'gyz'), may hold values from -8 to 60
Outputs:
- evolved: float32 [2, 12, 32, 32, 128], P(None, 'orb', 'gx', 'gyz'), parts along dimension 1
- residual: float32 [2, 12, 32, 32, 128], P(None, 'orb', 'gx', 'gyz'), parts along dimension 1
There are 4 independent parts, one for each index of `orb`. A program takes and returns all parts, laid end to end along the dimension named above; an argument that names none is the same for every part. Nothing has to cross between parts.
All inputs are finite; a program needn't handle non-finite values.
Results may differ from a plain program's by a relative error of at most 0.0003.
Values sent between devices are 32-bit elements; how exact they have to be, the bound alone decides.
A program may use at most 64 MiB of HBM per device.

v0:
```python
import jax
import jax.numpy as jnp
from jax import lax
from jax.sharding import PartitionSpec as P

ITERS = 4
SPACING = 0.25
HALF_STEP = 0.05
COEFF_NEAR = 4.0 / 3.0
COEFF_FAR = -1.0 / 12.0
COEFF_SELF = -2.5


def with_halo(array, sides, width):
    for axis, dim in sides:
        size, length = (lax.axis_size(axis), array.shape[dim])
        up = [(i, (i + 1) % size) for i in range(size - 1)]
        down = [(j, i) for i, j in up]
        last = lax.slice_in_dim(array, length - width, length, axis=dim)
        leading = lax.slice_in_dim(array, 0, width, axis=dim)
        before = lax.ppermute(last, axis, up)
        after = lax.ppermute(leading, axis, down)
        array = jnp.concatenate([before, array, after], axis=dim)
    return array


def laplace_apply(padded, potential):
    extent = (padded.shape[2] - 4, padded.shape[3] - 4, padded.shape[4] - 4)

    def window(shift_x, shift_y, shift_z):
        return padded[
            :,
            :,
            2 + shift_x : 2 + shift_x + extent[0],
            2 + shift_y : 2 + shift_y + extent[1],
            2 + shift_z : 2 + shift_z + extent[2],
        ]

    center = window(0, 0, 0)
    summed = 3.0 * COEFF_SELF * center
    for offset, weight in ((1, COEFF_NEAR), (2, COEFF_FAR)):
        summed = summed + weight * (
            window(offset, 0, 0)
            + window(-offset, 0, 0)
            + window(0, offset, 0)
            + window(0, -offset, 0)
            + window(0, 0, offset)
            + window(0, 0, -offset)
        )
    return -0.5 / SPACING**2 * summed + potential * center


def pad_depth(vector):
    return jnp.pad(vector, ((0, 0), (0, 0), (0, 0), (0, 0), (2, 2)))


def system(vector, applied):
    return jnp.stack([vector[0] - HALF_STEP * applied[1], vector[1] + HALF_STEP * applied[0]])


def precondition(vector, potential):
    diagonal = HALF_STEP * (3.75 / SPACING**2 + potential)
    divisor = 1.0 + diagonal * diagonal
    return jnp.stack(
        [(vector[0] + diagonal * vector[1]) / divisor, (vector[1] - diagonal * vector[0]) / divisor]
    )


def braket(left, right):
    real_part = jnp.sum(left[0] * right[0] + left[1] * right[1], axis=(1, 2, 3))
    imag_part = jnp.sum(left[0] * right[1] - left[1] * right[0], axis=(1, 2, 3))
    return (real_part, imag_part)


def times_complex(first, second):
    return (
        first[0] * second[0] - first[1] * second[1],
        first[0] * second[1] + first[1] * second[0],
    )


def divide_complex(first, second):
    modulus = second[0] * second[0] + second[1] * second[1]
    return (
        (first[0] * second[0] + first[1] * second[1]) / modulus,
        (first[1] * second[0] - first[0] * second[1]) / modulus,
    )


def scale_complex(coeff, vector):
    real_coef = coeff[0][:, None, None, None]
    imag_coef = coeff[1][:, None, None, None]
    return jnp.stack(
        [
            real_coef * vector[0] - imag_coef * vector[1],
            real_coef * vector[1] + imag_coef * vector[0],
        ]
    )


def shards(orbitals, potential):

    def apply_shallow(vector):
        padded = with_halo(vector, (("gx", 2), ("gyz", 3)), 2)
        return laplace_apply(pad_depth(padded), potential)

    h_orbitals = apply_shallow(orbitals)
    residual = jnp.stack([2.0 * HALF_STEP * h_orbitals[1], -2.0 * HALF_STEP * h_orbitals[0]])
    evolved = orbitals
    shadow = residual
    direction = residual
    rho_now = lax.psum(braket(shadow, residual), ("gx", "gyz"))
    for iteration in range(ITERS):
        dir_hat = precondition(direction, potential)
        image = system(dir_hat, apply_shallow(dir_hat))
        alpha_step = divide_complex(rho_now, lax.psum(braket(shadow, image), ("gx", "gyz")))
        half_step = residual - scale_complex(alpha_step, image)
        half_hat = precondition(half_step, potential)
        second = system(half_hat, apply_shallow(half_hat))
        cross_local = braket(second, half_step)
        norm_local = jnp.sum(second * second, axis=(0, 2, 3, 4))
        shadow_half = braket(shadow, half_step)
        shadow_second = braket(shadow, second)
        summed = lax.psum(
            (
                cross_local[0],
                cross_local[1],
                norm_local,
                shadow_half[0],
                shadow_half[1],
                shadow_second[0],
                shadow_second[1],
            ),
            ("gx", "gyz"),
        )
        cross_real, cross_imag, norm_second = (summed[0], summed[1], summed[2])
        omega_step = (cross_real / norm_second, cross_imag / norm_second)
        evolved = evolved + scale_complex(alpha_step, dir_hat) + scale_complex(omega_step, half_hat)
        residual = half_step - scale_complex(omega_step, second)
        if iteration + 1 < ITERS:
            along_second = times_complex(omega_step, (summed[5], summed[6]))
            rho_next = (summed[3] - along_second[0], summed[4] - along_second[1])
            beta_step = times_complex(
                divide_complex(rho_next, rho_now), divide_complex(alpha_step, omega_step)
            )
            direction = residual + scale_complex(
                beta_step, direction - scale_complex(omega_step, image)
            )
            rho_now = rho_next
    return (evolved, residual)


def solution(mesh):
    return jax.shard_map(
        shards,
        mesh=mesh,
        in_specs=(P(None, "orb", "gx", "gyz", None), P("gx", "gyz", None)),
        out_specs=(P(None, "orb", "gx", "gyz", None), P(None, "orb", "gx", "gyz", None)),
        check_vma=False,
    )
```

profile of v0, /device:TPU:0, one launch (start us, length us, event | category | flops | bytes accessed | tf_op | source)
XLA Modules:
  0.0 354.6 jit_solution(2603612143626635180)
XLA Ops:
  1.5 4.9 %collective-permute-start.1 = (f32[2,3,2,8,128]{4,3,2,1,0:T(8,128)S(1)}, f32[2,3,2,8,128]{4,3,2,1,0:T(8,128)S(1)}, u32[]{:S(2)}, u32[]{:S(2)}) collective-permute-start(f32[2,3,2,8,128]{4,3,2,1,0:T(8,128)S(1)} %get-tuple-element.244), channel_id=1, source_target_pairs={{0,4},{1,5},{2,6},{3,7},{8,12},{9,13},{10,14},{11,15},{16,20},{17,... | collective-permute-start | bytes 147464 | tf_op jit(solution)/shard_map/ppermute | solution.py:21
  6.4 1.3 collective-permute-start
  9.3 3.1 collective-permute-done
  12.5 3.5 collective-permute-start.3
  16.0 1.3 collective-permute-start.2
  18.4 4.4 %collective-permute-done.2 = f32[2,3,20,2,128]{4,3,2,1,0:T(2,128)S(1)} collective-permute-done((f32[2,3,20,2,128]{4,3,2,1,0:T(2,128)S(1)}, f32[2,3,20,2,128]{4,3,2,1,0:T(2,128)S(1)}, u32[]{:S(2)}, u32[]{:S(2)}) %collective-permute-start.2) | collective-permute-done | bytes 122912 | tf_op jit(solution)/shard_map/ppermute | solution.py:22
  24.6 1.6 collective-permute-start.5
  26.2 1.3 collective-permute-start.4
  27.9 4.3 %collective-permute-done.4 = f32[2,3,2,8,128]{4,3,2,1,0:T(8,128)S(1)} collective-permute-done((f32[2,3,2,8,128]{4,3,2,1,0:T(8,128)S(1)}, f32[2,3,2,8,128]{4,3,2,1,0:T(8,128)S(1)}, u32[]{:S(2)}, u32[]{:S(2)}) %collective-permute-start.4) | collective-permute-done | bytes 49184 | tf_op jit(solution)/shard_map/ppermute | solution.py:22
  32.2 3.5 collective-permute-start.7
  35.7 1.3 collective-permute-start.6
  38.2 4.4 %collective-permute-done.6 = f32[2,3,20,2,128]{4,3,2,1,0:T(2,128)S(1)} collective-permute-done((f32[2,3,20,2,128]{4,3,2,1,0:T(2,128)S(1)}, f32[2,3,20,2,128]{4,3,2,1,0:T(2,128)S(1)}, u32[]{:S(2)}, u32[]{:S(2)}) %collective-permute-start.6) | collective-permute-done | bytes 122912 | tf_op jit(solution)/shard_map/ppermute | solution.py:22
  44.6 18.8 %all-reduce.16 = (f32[3]{0:T(128)S(1)}, f32[3]{0:T(128)S(1)}, f32[3]{0:T(128)S(1)}, f32[3]{0:T(128)S(1)}) all-reduce(f32[3]{0:T(128)S(1)} %get-tuple-element.43, f32[3]{0:T(128)S(1)} %get-tuple-element.3, f32[3]{0:T(128)S(1)} %get-tuple-element.42, f32[3]{0:T(128)S(1)} %get-tuple-element.2), channel_id=1, replica_groups=mesh['orb'=4,'gx'=2,'gyz'=4] {'gx','gyz'}, use_global_device_ids=true, to_apply=%region_1.2 | all-reduce | flops 12 | bytes 96 | tf_op jit(solution)/shard_map/psum | solution.py:112
  64.5 1.8 collective-permute-start.9
  66.3 1.3 collective-permute-start.8
  68.0 4.3 %collective-permute-done.8 = f32[2,3,2,8,128]{4,3,2,1,0:T(8,128)S(1)} collective-permute-done((f32[2,3,2,8,128]{4,3,2,1,0:T(8,128)S(1)}, f32[2,3,2,8,128]{4,3,2,1,0:T(8,128)S(1)}, u32[]{:S(2)}, u32[]{:S(2)}) %collective-permute-start.8) | collective-permute-done | bytes 49184 | tf_op jit(solution)/shard_map/ppermute | solution.py:22
  72.4 2.1 collective-permute-start.11
  74.5 1.3 collective-permute-start.10
  76.9 4.4 %collective-permute-done.10 = f32[2,3,20,2,128]{4,3,2,1,0:T(2,128)S(1)} collective-permute-done((f32[2,3,20,2,128]{4,3,2,1,0:T(2,128)S(1)}, f32[2,3,20,2,128]{4,3,2,1,0:T(2,128)S(1)}, u32[]{:S(2)}, u32[]{:S(2)}) %collective-permute-start.10) | collective-permute-done | bytes 122912 | tf_op jit(solution)/shard_map/ppermute | solution.py:22
  83.6 17.2 %all-reduce.15 = (f32[3]{0:T(128)S(1)}, f32[3]{0:T(128)S(1)}, f32[3]{0:T(128)S(1)}, f32[3]{0:T(128)S(1)}, f32[3]{0:T(128)S(1)}, /*index=5*/f32[3]{0:T(128)S(1)}, f32[3]{0:T(128)S(1)}) all-reduce(f32[3]{0:T(128)S(1)} %get-tuple-element.40, f32[3]{0:T(128)S(1)} %fusion.80, ...), channel_id=1, replica_groups=mesh['orb'=4,'gx'=2,'gyz'=4] {'gx','gyz'}, use_global_device_ids=true, to_apply=%region_13.14 | all-reduce | flops 21 | bytes 168 | tf_op jit(solution)/shard_map/psum | solution.py:124
  102.9 3.8 %collective-permute-start.13 = (f32[2,3,2,8,128]{4,3,2,1,0:T(8,128)S(1)}, f32[2,3,2,8,128]{4,3,2,1,0:T(8,128)S(1)}, u32[]{:S(2)}, u32[]{:S(2)}) collective-permute-start(f32[2,3,2,8,128]{4,3,2,1,0:T(8,128)S(1)} %get-tuple-element.226), channel_id=1, source_target_pairs={{0,4},{1,5},{2,6},{3,7},{8,12},{9,13},{10,14},{11,15},{16,20},{17,... | collective-permute-start | bytes 147464 | tf_op jit(solution)/shard_map/ppermute | solution.py:21
  106.7 1.3 collective-permute-start.12
  108.5 4.3 %collective-permute-done.12 = f32[2,3,2,8,128]{4,3,2,1,0:T(8,128)S(1)} collective-permute-done((f32[2,3,2,8,128]{4,3,2,1,0:T(8,128)S(1)}, f32[2,3,2,8,128]{4,3,2,1,0:T(8,128)S(1)}, u32[]{:S(2)}, u32[]{:S(2)}) %collective-permute-start.12) | collective-permute-done | bytes 49184 | tf_op jit(solution)/shard_map/ppermute | solution.py:22
  112.8 1.7 collective-permute-start.15
  114.5 1.3 collective-permute-start.14
  116.9 4.4 %collective-permute-done.14 = f32[2,3,20,2,128]{4,3,2,1,0:T(2,128)S(1)} collective-permute-done((f32[2,3,20,2,128]{4,3,2,1,0:T(2,128)S(1)}, f32[2,3,20,2,128]{4,3,2,1,0:T(2,128)S(1)}, u32[]{:S(2)}, u32[]{:S(2)}) %collective-permute-start.14) | collective-permute-done | bytes 122912 | tf_op jit(solution)/shard_map/ppermute | solution.py:22
  123.3 17.2 %all-reduce.14 = (f32[3]{0:T(128)S(1)}, f32[3]{0:T(128)S(1)}) all-reduce(f32[3]{0:T(128)S(1)} %get-tuple-element.23, f32[3]{0:T(128)S(1)} %get-tuple-element.22), channel_id=1, replica_groups=mesh['orb'=4,'gx'=2,'gyz'=4] {'gx','gyz'}, use_global_device_ids=true, to_apply=%region_25.26 | all-reduce | flops 6 | bytes 48 | tf_op jit(solution)/shard_map/psum | solution.py:116
  142.2 3.8 %collective-permute-start.17 = (f32[2,3,2,8,128]{4,3,2,1,0:T(8,128)S(1)}, f32[2,3,2,8,128]{4,3,2,1,0:T(8,128)S(1)}, u32[]{:S(2)}, u32[]{:S(2)}) collective-permute-start(f32[2,3,2,8,128]{4,3,2,1,0:T(8,128)S(1)} %get-tuple-element.222), channel_id=1, source_target_pairs={{0,4},{1,5},{2,6},{3,7},{8,12},{9,13},{10,14},{11,15},{16,20},{17,... | collective-permute-start | bytes 147464 | tf_op jit(solution)/shard_map/ppermute | solution.py:21
  146.1 1.3 collective-permute-start.16
  147.8 4.3 %collective-permute-done.16 = f32[2,3,2,8,128]{4,3,2,1,0:T(8,128)S(1)} collective-permute-done((f32[2,3,2,8,128]{4,3,2,1,0:T(8,128)S(1)}, f32[2,3,2,8,128]{4,3,2,1,0:T(8,128)S(1)}, u32[]{:S(2)}, u32[]{:S(2)}) %collective-permute-start.16) | collective-permute-done | bytes 49184 | tf_op jit(solution)/shard_map/ppermute | solution.py:22
  152.1 1.7 collective-permute-start.19
  153.9 1.5 collective-permute-start.18
  156.3 4.4 %collective-permute-done.18 = f32[2,3,20,2,128]{4,3,2,1,0:T(2,128)S(1)} collective-permute-done((f32[2,3,20,2,128]{4,3,2,1,0:T(2,128)S(1)}, f32[2,3,20,2,128]{4,3,2,1,0:T(2,128)S(1)}, u32[]{:S(2)}, u32[]{:S(2)}) %collective-permute-start.18) | collective-permute-done | bytes 122912 | tf_op jit(solution)/shard_map/ppermute | solution.py:22
  163.6 17.4 %all-reduce.13 = (f32[3]{0:T(128)S(1)}, f32[3]{0:T(128)S(1)}, f32[3]{0:T(128)S(1)}, f32[3]{0:T(128)S(1)}, f32[3]{0:T(128)S(1)}, /*index=5*/f32[3]{0:T(128)S(1)}, f32[3]{0:T(128)S(1)}) all-reduce(f32[3]{0:T(128)} %get-tuple-element.36, f32[3]{0:T(128)S(1)} %fusion.81, ...), channel_id=1, replica_groups=mesh['orb'=4,'gx'=2,'gyz'=4] {'gx','gyz'}, use_global_device_ids=true, to_apply=%region_31.32 | all-reduce | flops 21 | bytes 168 | tf_op jit(solution)/shard_map/psum | solution.py:124
  181.7 1.9 multiply_subtract_fusion.12
  185.6 3.9 %collective-permute-start.21 = (f32[2,3,2,8,128]{4,3,2,1,0:T(8,128)S(1)}, f32[2,3,2,8,128]{4,3,2,1,0:T(8,128)S(1)}, u32[]{:S(2)}, u32[]{:S(2)}) collective-permute-start(f32[2,3,2,8,128]{4,3,2,1,0:T(8,128)S(1)} %get-tuple-element.216), channel_id=1, source_target_pairs={{0,4},{1,5},{2,6},{3,7},{8,12},{9,13},{10,14},{11,15},{16,20},{17,... | collective-permute-start | bytes 147464 | tf_op jit(solution)/shard_map/ppermute | solution.py:21
  189.6 1.3 collective-permute-start.20
  191.3 4.3 %collective-permute-done.20 = f32[2,3,2,8,128]{4,3,2,1,0:T(8,128)S(1)} collective-permute-done((f32[2,3,2,8,128]{4,3,2,1,0:T(8,128)S(1)}, f32[2,3,2,8,128]{4,3,2,1,0:T(8,128)S(1)}, u32[]{:S(2)}, u32[]{:S(2)}) %collective-permute-start.20) | collective-permute-done | bytes 49184 | tf_op jit(solution)/shard_map/ppermute | solution.py:22
  195.6 1.5 collective-permute-start.23
  197.1 1.3 collective-permute-start.22
  199.5 4.4 %collective-permute-done.22 = f32[2,3,20,2,128]{4,3,2,1,0:T(2,128)S(1)} collective-permute-done((f32[2,3,20,2,128]{4,3,2,1,0:T(2,128)S(1)}, f32[2,3,20,2,128]{4,3,2,1,0:T(2,128)S(1)}, u32[]{:S(2)}, u32[]{:S(2)}) %collective-permute-start.22) | collective-permute-done | bytes 122912 | tf_op jit(solution)/shard_map/ppermute | solution.py:22
  205.9 17.3 %all-reduce.12 = (f32[3]{0:T(128)S(1)}, f32[3]{0:T(128)S(1)}) all-reduce(f32[3]{0:T(128)S(1)} %get-tuple-element.15, f32[3]{0:T(128)S(1)} %get-tuple-element.14), channel_id=1, replica_groups=mesh['orb'=4,'gx'=2,'gyz'=4] {'gx','gyz'}, use_global_device_ids=true, to_apply=%region_43.44 | all-reduce | flops 6 | bytes 48 | tf_op jit(solution)/shard_map/psum | solution.py:116
  225.0 3.8 %collective-permute-start.25 = (f32[2,3,2,8,128]{4,3,2,1,0:T(8,128)S(1)}, f32[2,3,2,8,128]{4,3,2,1,0:T(8,128)S(1)}, u32[]{:S(2)}, u32[]{:S(2)}) collective-permute-start(f32[2,3,2,8,128]{4,3,2,1,0:T(8,128)S(1)} %get-tuple-element.212), channel_id=1, source_target_pairs={{0,4},{1,5},{2,6},{3,7},{8,12},{9,13},{10,14},{11,15},{16,20},{17,... | collective-permute-start | bytes 147464 | tf_op jit(solution)/shard_map/ppermute | solution.py:21
  230.6 4.3 %collective-permute-done.24 = f32[2,3,2,8,128]{4,3,2,1,0:T(8,128)S(1)} collective-permute-done((f32[2,3,2,8,128]{4,3,2,1,0:T(8,128)S(1)}, f32[2,3,2,8,128]{4,3,2,1,0:T(8,128)S(1)}, u32[]{:S(2)}, u32[]{:S(2)}) %collective-permute-start.24) | collective-permute-done | bytes 49184 | tf_op jit(solution)/shard_map/ppermute | solution.py:22
  235.0 1.6 collective-permute-start.27
  236.6 1.3 collective-permute-start.26
  239.0 4.6 %collective-permute-done.26 = f32[2,3,20,2,128]{4,3,2,1,0:T(2,128)S(1)} collective-permute-done((f32[2,3,20,2,128]{4,3,2,1,0:T(2,128)S(1)}, f32[2,3,20,2,128]{4,3,2,1,0:T(2,128)S(1)}, u32[]{:S(2)}, u32[]{:S(2)}) %collective-permute-start.26) | collective-permute-done | bytes 122912 | tf_op jit(solution)/shard_map/ppermute | solution.py:22
  247.1 18.0 %all-reduce.11 = (f32[3]{0:T(128)}, f32[3]{0:T(128)}, f32[3]{0:T(128)}, f32[3]{0:T(128)}, f32[3]{0:T(128)}, /*index=5*/f32[3]{0:T(128)}, f32[3]{0:T(128)}) all-reduce(f32[3]{0:T(128)} %get-tuple-element.32, f32[3]{0:T(128)} %fusion.82, f32[3]{0:T(128)} %get-tuple-element.33, ...), channel_id=1, replica_groups=mesh['orb'=4,'gx'=2,'gyz'=4] {'gx','gyz'}, use_global_device_ids=true, to_apply=%region_49.50 | all-reduce | flops 21 | bytes 168 | tf_op jit(solution)/shard_map/psum | solution.py:124
  265.0 1.3 multiply_subtract_fusion.22
  266.4 2.2 multiply_subtract_fusion.6
  269.5 3.8 %collective-permute-start.29 = (f32[2,3,2,8,128]{4,3,2,1,0:T(8,128)S(1)}, f32[2,3,2,8,128]{4,3,2,1,0:T(8,128)S(1)}, u32[]{:S(2)}, u32[]{:S(2)}) collective-permute-start(f32[2,3,2,8,128]{4,3,2,1,0:T(8,128)S(1)} %get-tuple-element.206), channel_id=1, source_target_pairs={{0,4},{1,5},{2,6},{3,7},{8,12},{9,13},{10,14},{11,15},{16,20},{17,... | collective-permute-start | bytes 147464 | tf_op jit(solution)/shard_map/ppermute | solution.py:21
  273.3 1.3 collective-permute-start.28
  275.1 4.3 %collective-permute-done.28 = f32[2,3,2,8,128]{4,3,2,1,0:T(8,128)S(1)} collective-permute-done((f32[2,3,2,8,128]{4,3,2,1,0:T(8,128)S(1)}, f32[2,3,2,8,128]{4,3,2,1,0:T(8,128)S(1)}, u32[]{:S(2)}, u32[]{:S(2)}) %collective-permute-start.28) | collective-permute-done | bytes 49184 | tf_op jit(solution)/shard_map/ppermute | solution.py:22
  279.4 1.7 collective-permute-start.31
  283.5 4.4 %collective-permute-done.30 = f32[2,3,20,2,128]{4,3,2,1,0:T(2,128)S(1)} collective-permute-done((f32[2,3,20,2,128]{4,3,2,1,0:T(2,128)S(1)}, f32[2,3,20,2,128]{4,3,2,1,0:T(2,128)S(1)}, u32[]{:S(2)}, u32[]{:S(2)}) %collective-permute-start.30) | collective-permute-done | bytes 122912 | tf_op jit(solution)/shard_map/ppermute | solution.py:22
  290.4 17.4 %all-reduce.10 = (f32[3]{0:T(128)S(1)}, f32[3]{0:T(128)S(1)}) all-reduce(f32[3]{0:T(128)S(1)} %get-tuple-element.7, f32[3]{0:T(128)S(1)} %get-tuple-element.6), channel_id=1, replica_groups=mesh['orb'=4,'gx'=2,'gyz'=4] {'gx','gyz'}, use_global_device_ids=true, to_apply=%region_61.62 | all-reduce | flops 6 | bytes 48 | tf_op jit(solution)/shard_map/psum | solution.py:116
  307.8 1.9 multiply_subtract_fusion.2
  311.7 3.8 %collective-permute-start.33 = (f32[2,3,2,8,128]{4,3,2,1,0:T(8,128)S(1)}, f32[2,3,2,8,128]{4,3,2,1,0:T(8,128)S(1)}, u32[]{:S(2)}, u32[]{:S(2)}) collective-permute-start(f32[2,3,2,8,128]{4,3,2,1,0:T(8,128)S(1)} %get-tuple-element.202), channel_id=1, source_target_pairs={{0,4},{1,5},{2,6},{3,7},{8,12},{9,13},{10,14},{11,15},{16,20},{17,... | collective-permute-start | bytes 147464 | tf_op jit(solution)/shard_map/ppermute | solution.py:21
  315.5 1.3 collective-permute-start.32
  317.2 4.3 %collective-permute-done.32 = f32[2,3,2,8,128]{4,3,2,1,0:T(8,128)S(1)} collective-permute-done((f32[2,3,2,8,128]{4,3,2,1,0:T(8,128)S(1)}, f32[2,3,2,8,128]{4,3,2,1,0:T(8,128)S(1)}, u32[]{:S(2)}, u32[]{:S(2)}) %collective-permute-start.32) | collective-permute-done | bytes 49184 | tf_op jit(solution)/shard_map/ppermute | solution.py:22
  321.6 1.7 collective-permute-start.35
  325.7 4.4 %collective-permute-done.34 = f32[2,3,20,2,128]{4,3,2,1,0:T(2,128)S(1)} collective-permute-done((f32[2,3,20,2,128]{4,3,2,1,0:T(2,128)S(1)}, f32[2,3,20,2,128]{4,3,2,1,0:T(2,128)S(1)}, u32[]{:S(2)}, u32[]{:S(2)}) %collective-permute-start.34) | collective-permute-done | bytes 122912 | tf_op jit(solution)/shard_map/ppermute | solution.py:22
  332.9 17.2 %all-reduce.9 = (f32[3]{0:T(128)S(1)}, f32[3]{0:T(128)S(1)}, f32[3]{0:T(128)S(1)}) all-reduce(f32[3]{0:T(128)S(1)} %get-tuple-element.5, f32[3]{0:T(128)S(1)} %fusion.83, f32[3]{0:T(128)S(1)} %get-tuple-element.4), channel_id=1, replica_groups=mesh['orb'=4,'gx'=2,'gyz'=4] {'gx','gyz'}, use_global_device_ids=true, to_apply=%region_67.68 | all-reduce | flops 9 | bytes 72 | tf_op jit(solution)/shard_map/psum | solution.py:124
  351.4 2.1 maximum_subtract_fusion.10
  (207 shorter events, 56.4 us)
Async XLA Ops:
  0.6 16.7 %copy-start = (f32[16,8,128]{2,1,0:T(8,128)S(1)}, f32[16,8,128]{2,1,0:T(8,128)}, u32[]{:S(2)}) copy-start(f32[16,8,128]{2,1,0:T(8,128)} %param.3) | copy-start | bytes 196612
  1.5 6.6 %collective-permute-start.1 = (f32[2,3,2,8,128]{4,3,2,1,0:T(8,128)S(1)}, f32[2,3,2,8,128]{4,3,2,1,0:T(8,128)S(1)}, u32[]{:S(2)}, u32[]{:S(2)}) collective-permute-start(f32[2,3,2,8,128]{4,3,2,1,0:T(8,128)S(1)} %get-tuple-element.244), channel_id=1, source_target_pairs={{0,4},{1,5},{2,6},{3,7},{8,12},{9,13},{10,14},{11,15},{16,20},{17,... | collective-permute-start | bytes 147464 | tf_op jit(solution)/shard_map/ppermute | solution.py:21
  6.4 6.0 %collective-permute-start = (f32[2,3,2,8,128]{4,3,2,1,0:T(8,128)S(1)}, f32[2,3,2,8,128]{4,3,2,1,0:T(8,128)S(1)}, u32[]{:S(2)}, u32[]{:S(2)}) collective-permute-start(f32[2,3,2,8,128]{4,3,2,1,0:T(8,128)S(1)} %get-tuple-element.243), channel_id=1, source_target_pairs={{4,0},{5,1},{6,2},{7,3},{12,8},{13,9},{14,10},{15,11},{20,16},{21,... | collective-permute-start | bytes 147464 | tf_op jit(solution)/shard_map/ppermute | solution.py:22
  9.2 14.6 %copy-start.1 = (f32[2,3,16,8,128]{4,3,2,1,0:T(8,128)S(1)}, f32[2,3,16,8,128]{4,3,2,1,0:T(8,128)}, u32[]{:S(2)}) copy-start(f32[2,3,16,8,128]{4,3,2,1,0:T(8,128)} %param.2) | copy-start | bytes 1179652
  12.5 5.9 %collective-permute-start.3 = (f32[2,3,20,2,128]{4,3,2,1,0:T(2,128)S(1)}, f32[2,3,20,2,128]{4,3,2,1,0:T(2,128)S(1)}, u32[]{:S(2)}, u32[]{:S(2)}) collective-permute-start(f32[2,3,20,2,128]{4,3,2,1,0:T(2,128)S(1)} %get-tuple-element.158), channel_id=1, source_target_pairs={{0,1},{1,2},{2,3},{4,5},{5,6},{6,7},{8,9},{9,10},{10,11},{12,13},{... | collective-permute-start | bytes 368648 | tf_op jit(solution)/shard_map/ppermute | solution.py:21
  16.0 6.8 %collective-permute-start.2 = (f32[2,3,20,2,128]{4,3,2,1,0:T(2,128)S(1)}, f32[2,3,20,2,128]{4,3,2,1,0:T(2,128)S(1)}, u32[]{:S(2)}, u32[]{:S(2)}) collective-permute-start(f32[2,3,20,2,128]{4,3,2,1,0:T(2,128)S(1)} %get-tuple-element.159), channel_id=1, source_target_pairs={{1,0},{2,1},{3,2},{5,4},{6,5},{7,6},{9,8},{10,9},{11,10},{13,12},{... | collective-permute-start | bytes 368648 | tf_op jit(solution)/shard_map/ppermute | solution.py:22
  24.6 3.3 collective-permute-start.5
  26.2 6.0 %collective-permute-start.4 = (f32[2,3,2,8,128]{4,3,2,1,0:T(8,128)S(1)}, f32[2,3,2,8,128]{4,3,2,1,0:T(8,128)S(1)}, u32[]{:S(2)}, u32[]{:S(2)}) collective-permute-start(f32[2,3,2,8,128]{4,3,2,1,0:T(8,128)S(1)} %get-tuple-element.239), channel_id=1, source_target_pairs={{4,0},{5,1},{6,2},{7,3},{12,8},{13,9},{14,10},{15,11},{20,16},{21,... | collective-permute-start | bytes 147464 | tf_op jit(solution)/shard_map/ppermute | solution.py:22
  32.2 5.9 %collective-permute-start.7 = (f32[2,3,20,2,128]{4,3,2,1,0:T(2,128)S(1)}, f32[2,3,20,2,128]{4,3,2,1,0:T(2,128)S(1)}, u32[]{:S(2)}, u32[]{:S(2)}) collective-permute-start(f32[2,3,20,2,128]{4,3,2,1,0:T(2,128)S(1)} %get-tuple-element.156), channel_id=1, source_target_pairs={{0,1},{1,2},{2,3},{4,5},{5,6},{6,7},{8,9},{9,10},{10,11},{12,13},{... | collective-permute-start | bytes 368648 | tf_op jit(solution)/shard_map/ppermute | solution.py:21
  35.7 6.8 %collective-permute-start.6 = (f32[2,3,20,2,128]{4,3,2,1,0:T(2,128)S(1)}, f32[2,3,20,2,128]{4,3,2,1,0:T(2,128)S(1)}, u32[]{:S(2)}, u32[]{:S(2)}) collective-permute-start(f32[2,3,20,2,128]{4,3,2,1,0:T(2,128)S(1)} %get-tuple-element.157), channel_id=1, source_target_pairs={{1,0},{2,1},{3,2},{5,4},{6,5},{7,6},{9,8},{10,9},{11,10},{13,12},{... | collective-permute-start | bytes 368648 | tf_op jit(solution)/shard_map/ppermute | solution.py:22
  64.5 3.6 %collective-permute-start.9 = (f32[2,3,2,8,128]{4,3,2,1,0:T(8,128)S(1)}, f32[2,3,2,8,128]{4,3,2,1,0:T(8,128)S(1)}, u32[]{:S(2)}, u32[]{:S(2)}) collective-permute-start(f32[2,3,2,8,128]{4,3,2,1,0:T(8,128)S(1)} %get-tuple-element.232), channel_id=1, source_target_pairs={{0,4},{1,5},{2,6},{3,7},{8,12},{9,13},{10,14},{11,15},{16,20},{17,... | collective-permute-start | bytes 147464 | tf_op jit(solution)/shard_map/ppermute | solution.py:21
  66.3 6.0 %collective-permute-start.8 = (f32[2,3,2,8,128]{4,3,2,1,0:T(8,128)S(1)}, f32[2,3,2,8,128]{4,3,2,1,0:T(8,128)S(1)}, u32[]{:S(2)}, u32[]{:S(2)}) collective-permute-start(f32[2,3,2,8,128]{4,3,2,1,0:T(8,128)S(1)} %get-tuple-element.233), channel_id=1, source_target_pairs={{4,0},{5,1},{6,2},{7,3},{12,8},{13,9},{14,10},{15,11},{20,16},{21,... | collective-permute-start | bytes 147464 | tf_op jit(solution)/shard_map/ppermute | solution.py:22
  72.4 4.5 %collective-permute-start.11 = (f32[2,3,20,2,128]{4,3,2,1,0:T(2,128)S(1)}, f32[2,3,20,2,128]{4,3,2,1,0:T(2,128)S(1)}, u32[]{:S(2)}, u32[]{:S(2)}) collective-permute-start(f32[2,3,20,2,128]{4,3,2,1,0:T(2,128)S(1)} %get-tuple-element.154), channel_id=1, source_target_pairs={{0,1},{1,2},{2,3},{4,5},{5,6},{6,7},{8,9},{9,10},{10,11},{12,13},{... | collective-permute-start | bytes 368648 | tf_op jit(solution)/shard_map/ppermute | solution.py:21
  74.5 6.8 %collective-permute-start.10 = (f32[2,3,20,2,128]{4,3,2,1,0:T(2,128)S(1)}, f32[2,3,20,2,128]{4,3,2,1,0:T(2,128)S(1)}, u32[]{:S(2)}, u32[]{:S(2)}) collective-permute-start(f32[2,3,20,2,128]{4,3,2,1,0:T(2,128)S(1)} %get-tuple-element.155), channel_id=1, source_target_pairs={{1,0},{2,1},{3,2},{5,4},{6,5},{7,6},{9,8},{10,9},{11,10},{13,12},{... | collective-permute-start | bytes 368648 | tf_op jit(solution)/shard_map/ppermute | solution.py:22
  100.9 39.6 %copy-start.34 = (f32[3]{0:T(128)}, f32[3]{0:T(128)S(1)}, u32[]{:S(2)}) copy-start(f32[3]{0:T(128)S(1)} %get-tuple-element.107) | copy-start | bytes 40
  100.9 39.6 %copy-start.35 = (f32[3]{0:T(128)}, f32[3]{0:T(128)S(1)}, u32[]{:S(2)}) copy-start(f32[3]{0:T(128)S(1)} %get-tuple-element.108) | copy-start | bytes 40
  102.1 0.8 copy-start.13
  102.9 5.5 %collective-permute-start.13 = (f32[2,3,2,8,128]{4,3,2,1,0:T(8,128)S(1)}, f32[2,3,2,8,128]{4,3,2,1,0:T(8,128)S(1)}, u32[]{:S(2)}, u32[]{:S(2)}) collective-permute-start(f32[2,3,2,8,128]{4,3,2,1,0:T(8,128)S(1)} %get-tuple-element.226), channel_id=1, source_target_pairs={{0,4},{1,5},{2,6},{3,7},{8,12},{9,13},{10,14},{11,15},{16,20},{17,... | collective-permute-start | bytes 147464 | tf_op jit(solution)/shard_map/ppermute | solution.py:21
  106.7 6.0 %collective-permute-start.12 = (f32[2,3,2,8,128]{4,3,2,1,0:T(8,128)S(1)}, f32[2,3,2,8,128]{4,3,2,1,0:T(8,128)S(1)}, u32[]{:S(2)}, u32[]{:S(2)}) collective-permute-start(f32[2,3,2,8,128]{4,3,2,1,0:T(8,128)S(1)} %get-tuple-element.227), channel_id=1, source_target_pairs={{4,0},{5,1},{6,2},{7,3},{12,8},{13,9},{14,10},{15,11},{20,16},{21,... | collective-permute-start | bytes 147464 | tf_op jit(solution)/shard_map/ppermute | solution.py:22
  112.8 4.1 %collective-permute-start.15 = (f32[2,3,20,2,128]{4,3,2,1,0:T(2,128)S(1)}, f32[2,3,20,2,128]{4,3,2,1,0:T(2,128)S(1)}, u32[]{:S(2)}, u32[]{:S(2)}) collective-permute-start(f32[2,3,20,2,128]{4,3,2,1,0:T(2,128)S(1)} %get-tuple-element.152), channel_id=1, source_target_pairs={{0,1},{1,2},{2,3},{4,5},{5,6},{6,7},{8,9},{9,10},{10,11},{12,13},{... | collective-permute-start | bytes 368648 | tf_op jit(solution)/shard_map/ppermute | solution.py:21
  114.5 6.8 %collective-permute-start.14 = (f32[2,3,20,2,128]{4,3,2,1,0:T(2,128)S(1)}, f32[2,3,20,2,128]{4,3,2,1,0:T(2,128)S(1)}, u32[]{:S(2)}, u32[]{:S(2)}) collective-permute-start(f32[2,3,20,2,128]{4,3,2,1,0:T(2,128)S(1)} %get-tuple-element.153), channel_id=1, source_target_pairs={{1,0},{2,1},{3,2},{5,4},{6,5},{7,6},{9,8},{10,9},{11,10},{13,12},{... | collective-permute-start | bytes 368648 | tf_op jit(solution)/shard_map/ppermute | solution.py:22
  142.2 5.6 %collective-permute-start.17 = (f32[2,3,2,8,128]{4,3,2,1,0:T(8,128)S(1)}, f32[2,3,2,8,128]{4,3,2,1,0:T(8,128)S(1)}, u32[]{:S(2)}, u32[]{:S(2)}) collective-permute-start(f32[2,3,2,8,128]{4,3,2,1,0:T(8,128)S(1)} %get-tuple-element.222), channel_id=1, source_target_pairs={{0,4},{1,5},{2,6},{3,7},{8,12},{9,13},{10,14},{11,15},{16,20},{17,... | collective-permute-start | bytes 147464 | tf_op jit(solution)/shard_map/ppermute | solution.py:21
  146.1 6.0 %collective-permute-start.16 = (f32[2,3,2,8,128]{4,3,2,1,0:T(8,128)S(1)}, f32[2,3,2,8,128]{4,3,2,1,0:T(8,128)S(1)}, u32[]{:S(2)}, u32[]{:S(2)}) collective-permute-start(f32[2,3,2,8,128]{4,3,2,1,0:T(8,128)S(1)} %get-tuple-element.223), channel_id=1, source_target_pairs={{4,0},{5,1},{6,2},{7,3},{12,8},{13,9},{14,10},{15,11},{20,16},{21,... | collective-permute-start | bytes 147464 | tf_op jit(solution)/shard_map/ppermute | solution.py:22
  152.1 4.2 %collective-permute-start.19 = (f32[2,3,20,2,128]{4,3,2,1,0:T(2,128)S(1)}, f32[2,3,20,2,128]{4,3,2,1,0:T(2,128)S(1)}, u32[]{:S(2)}, u32[]{:S(2)}) collective-permute-start(f32[2,3,20,2,128]{4,3,2,1,0:T(2,128)S(1)} %get-tuple-element.150), channel_id=1, source_target_pairs={{0,1},{1,2},{2,3},{4,5},{5,6},{6,7},{8,9},{9,10},{10,11},{12,13},{... | collective-permute-start | bytes 368648 | tf_op jit(solution)/shard_map/ppermute | solution.py:21
  153.9 6.8 %collective-permute-start.18 = (f32[2,3,20,2,128]{4,3,2,1,0:T(2,128)S(1)}, f32[2,3,20,2,128]{4,3,2,1,0:T(2,128)S(1)}, u32[]{:S(2)}, u32[]{:S(2)}) collective-permute-start(f32[2,3,20,2,128]{4,3,2,1,0:T(2,128)S(1)} %get-tuple-element.151), channel_id=1, source_target_pairs={{1,0},{2,1},{3,2},{5,4},{6,5},{7,6},{9,8},{10,9},{11,10},{13,12},{... | collective-permute-start | bytes 368648 | tf_op jit(solution)/shard_map/ppermute | solution.py:22
  185.6 5.7 %collective-permute-start.21 = (f32[2,3,2,8,128]{4,3,2,1,0:T(8,128)S(1)}, f32[2,3,2,8,128]{4,3,2,1,0:T(8,128)S(1)}, u32[]{:S(2)}, u32[]{:S(2)}) collective-permute-start(f32[2,3,2,8,128]{4,3,2,1,0:T(8,128)S(1)} %get-tuple-element.216), channel_id=1, source_target_pairs={{0,4},{1,5},{2,6},{3,7},{8,12},{9,13},{10,14},{11,15},{16,20},{17,... | collective-permute-start | bytes 147464 | tf_op jit(solution)/shard_map/ppermute | solution.py:21
  189.6 6.0 %collective-permute-start.20 = (f32[2,3,2,8,128]{4,3,2,1,0:T(8,128)S(1)}, f32[2,3,2,8,128]{4,3,2,1,0:T(8,128)S(1)}, u32[]{:S(2)}, u32[]{:S(2)}) collective-permute-start(f32[2,3,2,8,128]{4,3,2,1,0:T(8,128)S(1)} %get-tuple-element.217), channel_id=1, source_target_pairs={{4,0},{5,1},{6,2},{7,3},{12,8},{13,9},{14,10},{15,11},{20,16},{21,... | collective-permute-start | bytes 147464 | tf_op jit(solution)/shard_map/ppermute | solution.py:22
  195.6 3.9 %collective-permute-start.23 = (f32[2,3,20,2,128]{4,3,2,1,0:T(2,128)S(1)}, f32[2,3,20,2,128]{4,3,2,1,0:T(2,128)S(1)}, u32[]{:S(2)}, u32[]{:S(2)}) collective-permute-start(f32[2,3,20,2,128]{4,3,2,1,0:T(2,128)S(1)} %get-tuple-element.148), channel_id=1, source_target_pairs={{0,1},{1,2},{2,3},{4,5},{5,6},{6,7},{8,9},{9,10},{10,11},{12,13},{... | collective-permute-start | bytes 368648 | tf_op jit(solution)/shard_map/ppermute | solution.py:21
  197.1 6.8 %collective-permute-start.22 = (f32[2,3,20,2,128]{4,3,2,1,0:T(2,128)S(1)}, f32[2,3,20,2,128]{4,3,2,1,0:T(2,128)S(1)}, u32[]{:S(2)}, u32[]{:S(2)}) collective-permute-start(f32[2,3,20,2,128]{4,3,2,1,0:T(2,128)S(1)} %get-tuple-element.149), channel_id=1, source_target_pairs={{1,0},{2,1},{3,2},{5,4},{6,5},{7,6},{9,8},{10,9},{11,10},{13,12},{... | collective-permute-start | bytes 368648 | tf_op jit(solution)/shard_map/ppermute | solution.py:22
  224.1 0.8 copy-start.10
  225.0 5.6 %collective-permute-start.25 = (f32[2,3,2,8,128]{4,3,2,1,0:T(8,128)S(1)}, f32[2,3,2,8,128]{4,3,2,1,0:T(8,128)S(1)}, u32[]{:S(2)}, u32[]{:S(2)}) collective-permute-start(f32[2,3,2,8,128]{4,3,2,1,0:T(8,128)S(1)} %get-tuple-element.212), channel_id=1, source_target_pairs={{0,4},{1,5},{2,6},{3,7},{8,12},{9,13},{10,14},{11,15},{16,20},{17,... | collective-permute-start | bytes 147464 | tf_op jit(solution)/shard_map/ppermute | solution.py:21
  228.9 6.0 %collective-permute-start.24 = (f32[2,3,2,8,128]{4,3,2,1,0:T(8,128)S(1)}, f32[2,3,2,8,128]{4,3,2,1,0:T(8,128)S(1)}, u32[]{:S(2)}, u32[]{:S(2)}) collective-permute-start(f32[2,3,2,8,128]{4,3,2,1,0:T(8,128)S(1)} %get-tuple-element.213), channel_id=1, source_target_pairs={{4,0},{5,1},{6,2},{7,3},{12,8},{13,9},{14,10},{15,11},{20,16},{21,... | collective-permute-start | bytes 147464 | tf_op jit(solution)/shard_map/ppermute | solution.py:22
  235.0 4.0 %collective-permute-start.27 = (f32[2,3,20,2,128]{4,3,2,1,0:T(2,128)S(1)}, f32[2,3,20,2,128]{4,3,2,1,0:T(2,128)S(1)}, u32[]{:S(2)}, u32[]{:S(2)}) collective-permute-start(f32[2,3,20,2,128]{4,3,2,1,0:T(2,128)S(1)} %get-tuple-element.146), channel_id=1, source_target_pairs={{0,1},{1,2},{2,3},{4,5},{5,6},{6,7},{8,9},{9,10},{10,11},{12,13},{... | collective-permute-start | bytes 368648 | tf_op jit(solution)/shard_map/ppermute | solution.py:21
  236.6 7.0 %collective-permute-start.26 = (f32[2,3,20,2,128]{4,3,2,1,0:T(2,128)S(1)}, f32[2,3,20,2,128]{4,3,2,1,0:T(2,128)S(1)}, u32[]{:S(2)}, u32[]{:S(2)}) collective-permute-start(f32[2,3,20,2,128]{4,3,2,1,0:T(2,128)S(1)} %get-tuple-element.147), channel_id=1, source_target_pairs={{1,0},{2,1},{3,2},{5,4},{6,5},{7,6},{9,8},{10,9},{11,10},{13,12},{... | collective-permute-start | bytes 368648 | tf_op jit(solution)/shard_map/ppermute | solution.py:22
  245.5 1.0 copy-start.7
  245.5 20.9 %copy-start.6 = (f32[1,3,16,8,128]{4,3,2,1,0:T(8,128)}, f32[1,3,16,8,128]{4,3,2,1,0:T(8,128)S(1)}, u32[]{:S(2)}) copy-start(f32[1,3,16,8,128]{4,3,2,1,0:T(8,128)S(1)} %get-tuple-element.208) | copy-start | bytes 589828
  265.0 3.5 copy-start.15
  265.0 3.5 copy-start.17
  269.5 5.6 %collective-permute-start.29 = (f32[2,3,2,8,128]{4,3,2,1,0:T(8,128)S(1)}, f32[2,3,2,8,128]{4,3,2,1,0:T(8,128)S(1)}, u32[]{:S(2)}, u32[]{:S(2)}) collective-permute-start(f32[2,3,2,8,128]{4,3,2,1,0:T(8,128)S(1)} %get-tuple-element.206), channel_id=1, source_target_pairs={{0,4},{1,5},{2,6},{3,7},{8,12},{9,13},{10,14},{11,15},{16,20},{17,... | collective-permute-start | bytes 147464 | tf_op jit(solution)/shard_map/ppermute | solution.py:21
  273.3 6.0 %collective-permute-start.28 = (f32[2,3,2,8,128]{4,3,2,1,0:T(8,128)S(1)}, f32[2,3,2,8,128]{4,3,2,1,0:T(8,128)S(1)}, u32[]{:S(2)}, u32[]{:S(2)}) collective-permute-start(f32[2,3,2,8,128]{4,3,2,1,0:T(8,128)S(1)} %get-tuple-element.207), channel_id=1, source_target_pairs={{4,0},{5,1},{6,2},{7,3},{12,8},{13,9},{14,10},{15,11},{20,16},{21,... | collective-permute-start | bytes 147464 | tf_op jit(solution)/shard_map/ppermute | solution.py:22
  279.4 4.1 %collective-permute-start.31 = (f32[2,3,20,2,128]{4,3,2,1,0:T(2,128)S(1)}, f32[2,3,20,2,128]{4,3,2,1,0:T(2,128)S(1)}, u32[]{:S(2)}, u32[]{:S(2)}) collective-permute-start(f32[2,3,20,2,128]{4,3,2,1,0:T(2,128)S(1)} %get-tuple-element.144), channel_id=1, source_target_pairs={{0,1},{1,2},{2,3},{4,5},{5,6},{6,7},{8,9},{9,10},{10,11},{12,13},{... | collective-permute-start | bytes 368648 | tf_op jit(solution)/shard_map/ppermute | solution.py:21
  281.1 6.8 %collective-permute-start.30 = (f32[2,3,20,2,128]{4,3,2,1,0:T(2,128)S(1)}, f32[2,3,20,2,128]{4,3,2,1,0:T(2,128)S(1)}, u32[]{:S(2)}, u32[]{:S(2)}) collective-permute-start(f32[2,3,20,2,128]{4,3,2,1,0:T(2,128)S(1)} %get-tuple-element.145), channel_id=1, source_target_pairs={{1,0},{2,1},{3,2},{5,4},{6,5},{7,6},{9,8},{10,9},{11,10},{13,12},{... | collective-permute-start | bytes 368648 | tf_op jit(solution)/shard_map/ppermute | solution.py:22
  289.6 18.2 %copy-start.36 = (f32[3]{0:T(128)S(1)}, f32[3]{0:T(128)}, u32[]{:S(2)}) copy-start(f32[3]{0:T(128)} %get-tuple-element.83) | copy-start | bytes 40
  289.6 18.2 %copy-start.37 = (f32[3]{0:T(128)S(1)}, f32[3]{0:T(128)}, u32[]{:S(2)}) copy-start(f32[3]{0:T(128)} %get-tuple-element.84) | copy-start | bytes 40
  311.7 5.6 %collective-permute-start.33 = (f32[2,3,2,8,128]{4,3,2,1,0:T(8,128)S(1)}, f32[2,3,2,8,128]{4,3,2,1,0:T(8,128)S(1)}, u32[]{:S(2)}, u32[]{:S(2)}) collective-permute-start(f32[2,3,2,8,128]{4,3,2,1,0:T(8,128)S(1)} %get-tuple-element.202), channel_id=1, source_target_pairs={{0,4},{1,5},{2,6},{3,7},{8,12},{9,13},{10,14},{11,15},{16,20},{17,... | collective-permute-start | bytes 147464 | tf_op jit(solution)/shard_map/ppermute | solution.py:21
  315.5 6.0 %collective-permute-start.32 = (f32[2,3,2,8,128]{4,3,2,1,0:T(8,128)S(1)}, f32[2,3,2,8,128]{4,3,2,1,0:T(8,128)S(1)}, u32[]{:S(2)}, u32[]{:S(2)}) collective-permute-start(f32[2,3,2,8,128]{4,3,2,1,0:T(8,128)S(1)} %get-tuple-element.203), channel_id=1, source_target_pairs={{4,0},{5,1},{6,2},{7,3},{12,8},{13,9},{14,10},{15,11},{20,16},{21,... | collective-permute-start | bytes 147464 | tf_op jit(solution)/shard_map/ppermute | solution.py:22
  321.6 4.1 %collective-permute-start.35 = (f32[2,3,20,2,128]{4,3,2,1,0:T(2,128)S(1)}, f32[2,3,20,2,128]{4,3,2,1,0:T(2,128)S(1)}, u32[]{:S(2)}, u32[]{:S(2)}) collective-permute-start(f32[2,3,20,2,128]{4,3,2,1,0:T(2,128)S(1)} %get-tuple-element.142), channel_id=1, source_target_pairs={{0,1},{1,2},{2,3},{4,5},{5,6},{6,7},{8,9},{9,10},{10,11},{12,13},{... | collective-permute-start | bytes 368648 | tf_op jit(solution)/shard_map/ppermute | solution.py:21
  323.2 6.8 %collective-permute-start.34 = (f32[2,3,20,2,128]{4,3,2,1,0:T(2,128)S(1)}, f32[2,3,20,2,128]{4,3,2,1,0:T(2,128)S(1)}, u32[]{:S(2)}, u32[]{:S(2)}) collective-permute-start(f32[2,3,20,2,128]{4,3,2,1,0:T(2,128)S(1)} %get-tuple-element.143), channel_id=1, source_target_pairs={{1,0},{2,1},{3,2},{5,4},{6,5},{7,6},{9,8},{10,9},{11,10},{13,12},{... | collective-permute-start | bytes 368648 | tf_op jit(solution)/shard_map/ppermute | solution.py:22
  331.7 19.4 %copy-start.5 = (f32[1,3,16,8,128]{4,3,2,1,0:T(8,128)S(1)}, f32[1,3,16,8,128]{4,3,2,1,0:T(8,128)}, u32[]{:S(2)}) copy-start(f32[1,3,16,8,128]{4,3,2,1,0:T(8,128)} %copy-done.4) | copy-start | bytes 589828
  351.2 2.3 copy-start.2
  351.2 2.3 copy-start.20
  351.2 2.3 copy-start.21
  351.2 2.3 copy-start.22
  351.2 2.3 copy-start.23
  351.3 2.3 copy-start.24
  351.3 2.3 copy-start.25
  351.3 2.3 copy-start.26
  351.3 2.3 copy-start.27
  351.3 2.3 copy-start.28
  351.3 2.3 copy-start.29
  351.3 2.3 copy-start.30
  351.3 2.3 copy-start.31
  351.3 2.3 copy-start.32
  351.3 2.3 copy-start.33
  (10 other events, 7.0 us)
where the time goes:
time: 356 us; the launch traced here: 355 us
  blocking collectives  141 us (40%)
  waiting for transfers between devices  89.8 us (25%)
  starting transfers between devices  73.6 us (21%)
  other arithmetic  41.9 us (12%)
  local copies, waits for them, and re-layouts  6.87 us (2%)
    ppermute x18, waiting for transfers between devices, with_halo(): after = lax.ppermute(leading, axis, down)  76.6 us
    psum x4, blocking collectives, shards(): lax.psum((cross_local[0], cross_local[1], norm_local, shadow_half[0], sha...  69.8 us
    psum x3, blocking collectives, shards(): lax.psum(braket(shadow, image), ('gx', 'gyz'))  51.9 us
    ppermute x18, starting transfers between devices, with_halo(): before = lax.ppermute(last, axis, up)  50.2 us
    ppermute x18, starting transfers between devices, with_halo(): after = lax.ppermute(leading, axis, down)  23.4 us
    psum x1, blocking collectives, shards(): rho_now = lax.psum(braket(shadow, residual), ('gx', 'gyz'))  18.8 us
    ppermute x18, waiting for transfers between devices, with_halo(): before = lax.ppermute(last, axis, up)  13.2 us
    sub x11, other arithmetic, scale_complex(): real_coef * vector[0] - imag_coef * vector[1]  11.1 us
  transfers between devices with their start and end apart: 36, of which 36 were waited for; matrix products, arithmetic and copies ran while one was open for 0% of the time, Pallas kernels for 0%

commit v1 on v0

--- a/solution.py
+++ b/solution.py
@@ -113,7 +113,7 @@
     for iteration in range(ITERS):
         dir_hat = precondition(direction, potential)
         image = system(dir_hat, apply_shallow(dir_hat))
-        alpha_step = divide_complex(rho_now, lax.psum(braket(shadow, image), ("gx", "gyz")))
+        alpha_step = divide_complex(rho_now, lax.psum(lax.psum(braket(shadow, image), "gyz"), "gx"))
         half_step = residual - scale_complex(alpha_step, image)
         half_hat = precondition(half_step, potential)
         second = system(half_hat, apply_shallow(half_hat))

time: 356 us -> 360 us (1.011)
    psum x3 -> x8, blocking collectives: 51.9 us -> 56.6 us  [the longest x4 37 us: shards(): lax.psum(braket(shadow, image), 'gyz')]
where the time goes in v1:
time: 360 us; the launch traced here: 359 us
  blocking collectives  144 us (40%)
  waiting for transfers between devices  90.5 us (25%)
  starting transfers between devices  73.6 us (20%)
  other arithmetic  42 us (12%)
  local copies, waits for them, and re-layouts  6.89 us (2%)
    ppermute x18, waiting for transfers between devices, with_halo(): after = lax.ppermute(leading, axis, down)  76.6 us
    psum x4, blocking collectives, shards(): lax.psum((cross_local[0], cross_local[1], norm_local, shadow_half[0], sha...  70 us
    ppermute x18, starting transfers between devices, with_halo(): before = lax.ppermute(last, axis, up)  49.9 us
    psum x4, blocking collectives, shards(): lax.psum(braket(shadow, image), 'gyz')  37 us
    ppermute x18, starting transfers between devices, with_halo(): after = lax.ppermute(leading, axis, down)  23.7 us
    psum x4, blocking collectives, shards(): lax.psum(lax.psum(braket(shadow, image), 'gyz'), 'gx')  19.7 us
    psum x1, blocking collectives, shards(): rho_now = lax.psum(braket(shadow, residual), ('gx', 'gyz'))  17.6 us
    ppermute x18, waiting for transfers between devices, with_halo(): before = lax.ppermute(last, axis, up)  13.9 us
  transfers between devices with their start and end apart: 36, of which 36 were waited for; matrix products, arithmetic and copies ran while one was open for 0% of the time, Pallas kernels for 0%

profile of v1, /device:TPU:0, one launch (start us, length us, event | category | flops | bytes accessed | tf_op | source)
XLA Modules:
  0.0 359.0 jit_solution(3986117640338845528)
XLA Ops:
  1.5 4.9 %collective-permute-start.1 = (f32[2,3,2,8,128]{4,3,2,1,0:T(8,128)S(1)}, f32[2,3,2,8,128]{4,3,2,1,0:T(8,128)S(1)}, u32[]{:S(2)}, u32[]{:S(2)}) collective-permute-start(f32[2,3,2,8,128]{4,3,2,1,0:T(8,128)S(1)} %get-tuple-element.252), channel_id=1, source_target_pairs={{0,4},{1,5},{2,6},{3,7},{8,12},{9,13},{10,14},{11,15},{16,20},{17,... | collective-permute-start | bytes 147464 | tf_op jit(solution)/shard_map/ppermute | solution.py:21
  6.4 1.3 collective-permute-start
  9.3 3.1 collective-permute-done
  12.5 3.5 collective-permute-start.3
  16.0 1.3 collective-permute-start.2
  18.4 4.4 %collective-permute-done.2 = f32[2,3,20,2,128]{4,3,2,1,0:T(2,128)S(1)} collective-permute-done((f32[2,3,20,2,128]{4,3,2,1,0:T(2,128)S(1)}, f32[2,3,20,2,128]{4,3,2,1,0:T(2,128)S(1)}, u32[]{:S(2)}, u32[]{:S(2)}) %collective-permute-start.2) | collective-permute-done | bytes 122912 | tf_op jit(solution)/shard_map/ppermute | solution.py:22
  24.6 1.6 collective-permute-start.5
  26.2 1.3 collective-permute-start.4
  27.9 4.3 %collective-permute-done.4 = f32[2,3,2,8,128]{4,3,2,1,0:T(8,128)S(1)} collective-permute-done((f32[2,3,2,8,128]{4,3,2,1,0:T(8,128)S(1)}, f32[2,3,2,8,128]{4,3,2,1,0:T(8,128)S(1)}, u32[]{:S(2)}, u32[]{:S(2)}) %collective-permute-start.4) | collective-permute-done | bytes 49184 | tf_op jit(solution)/shard_map/ppermute | solution.py:22
  32.2 3.5 collective-permute-start.7
  35.7 1.3 collective-permute-start.6
  38.2 4.4 %collective-permute-done.6 = f32[2,3,20,2,128]{4,3,2,1,0:T(2,128)S(1)} collective-permute-done((f32[2,3,20,2,128]{4,3,2,1,0:T(2,128)S(1)}, f32[2,3,20,2,128]{4,3,2,1,0:T(2,128)S(1)}, u32[]{:S(2)}, u32[]{:S(2)}) %collective-permute-start.6) | collective-permute-done | bytes 122912 | tf_op jit(solution)/shard_map/ppermute | solution.py:22
  44.6 9.9 %all-reduce.17 = (f32[3]{0:T(128)S(1)}, f32[3]{0:T(128)S(1)}) all-reduce(f32[3]{0:T(128)S(1)} %get-tuple-element.3, f32[3]{0:T(128)S(1)} %get-tuple-element.2), channel_id=1, replica_groups=mesh['orb'=4,'gx'=2,'gyz'=4] {'gyz'}, use_global_device_ids=true, to_apply=%region_8.9 | all-reduce | flops 6 | bytes 48 | tf_op jit(solution)/shard_map/psum | solution.py:116
  54.5 4.9 %all-reduce.21 = (f32[3]{0:T(128)S(1)}, f32[3]{0:T(128)S(1)}) all-reduce(f32[3]{0:T(128)S(1)} %get-tuple-element.76, f32[3]{0:T(128)S(1)} %get-tuple-element.77), channel_id=1, replica_groups=mesh['orb'=4,'gx'=2,'gyz'=4] {'gx'}, use_global_device_ids=true, to_apply=%region_9.10 | all-reduce | flops 6 | bytes 48 | tf_op jit(solution)/shard_map/psum | solution.py:116
  59.4 17.6 %all-reduce.13 = (f32[3]{0:T(128)S(1)}, f32[3]{0:T(128)S(1)}) all-reduce(f32[3]{0:T(128)S(1)} %get-tuple-element.43, f32[3]{0:T(128)S(1)} %get-tuple-element.42), channel_id=1, replica_groups=mesh['orb'=4,'gx'=2,'gyz'=4] {'gx','gyz'}, use_global_device_ids=true, to_apply=%region_1.2 | all-reduce | flops 6 | bytes 48 | tf_op jit(solution)/shard_map/psum | solution.py:112
  78.1 3.4 collective-permute-start.9
  81.5 1.3 collective-permute-start.8
  83.3 4.3 %collective-permute-done.8 = f32[2,3,2,8,128]{4,3,2,1,0:T(8,128)S(1)} collective-permute-done((f32[2,3,2,8,128]{4,3,2,1,0:T(8,128)S(1)}, f32[2,3,2,8,128]{4,3,2,1,0:T(8,128)S(1)}, u32[]{:S(2)}, u32[]{:S(2)}) %collective-permute-start.8) | collective-permute-done | bytes 49184 | tf_op jit(solution)/shard_map/ppermute | solution.py:22
  87.6 2.0 collective-permute-start.11
  89.6 1.3 collective-permute-start.10
  92.1 4.3 %collective-permute-done.10 = f32[2,3,20,2,128]{4,3,2,1,0:T(2,128)S(1)} collective-permute-done((f32[2,3,20,2,128]{4,3,2,1,0:T(2,128)S(1)}, f32[2,3,20,2,128]{4,3,2,1,0:T(2,128)S(1)}, u32[]{:S(2)}, u32[]{:S(2)}) %collective-permute-start.10) | collective-permute-done | bytes 122912 | tf_op jit(solution)/shard_map/ppermute | solution.py:22
  98.8 17.4 %all-reduce.12 = (f32[3]{0:T(128)S(1)}, f32[3]{0:T(128)S(1)}, f32[3]{0:T(128)S(1)}, f32[3]{0:T(128)S(1)}, f32[3]{0:T(128)S(1)}, /*index=5*/f32[3]{0:T(128)S(1)}, f32[3]{0:T(128)S(1)}) all-reduce(f32[3]{0:T(128)S(1)} %get-tuple-element.40, f32[3]{0:T(128)S(1)} %fusion.80, ...), channel_id=1, replica_groups=mesh['orb'=4,'gx'=2,'gyz'=4] {'gx','gyz'}, use_global_device_ids=true, to_apply=%region_15.16 | all-reduce | flops 21 | bytes 168 | tf_op jit(solution)/shard_map/psum | solution.py:124
  118.2 3.4 collective-permute-start.13
  123.4 4.3 %collective-permute-done.12 = f32[2,3,2,8,128]{4,3,2,1,0:T(8,128)S(1)} collective-permute-done((f32[2,3,2,8,128]{4,3,2,1,0:T(8,128)S(1)}, f32[2,3,2,8,128]{4,3,2,1,0:T(8,128)S(1)}, u32[]{:S(2)}, u32[]{:S(2)}) %collective-permute-start.12) | collective-permute-done | bytes 49184 | tf_op jit(solution)/shard_map/ppermute | solution.py:22
  127.7 1.8 collective-permute-start.15
  132.0 4.4 %collective-permute-done.14 = f32[2,3,20,2,128]{4,3,2,1,0:T(2,128)S(1)} collective-permute-done((f32[2,3,20,2,128]{4,3,2,1,0:T(2,128)S(1)}, f32[2,3,20,2,128]{4,3,2,1,0:T(2,128)S(1)}, u32[]{:S(2)}, u32[]{:S(2)}) %collective-permute-start.14) | collective-permute-done | bytes 122912 | tf_op jit(solution)/shard_map/ppermute | solution.py:22
  138.3 9.1 %all-reduce.16 = (f32[3]{0:T(128)S(1)}, f32[3]{0:T(128)S(1)}) all-reduce(f32[3]{0:T(128)S(1)} %get-tuple-element.23, f32[3]{0:T(128)S(1)} %get-tuple-element.22), channel_id=1, replica_groups=mesh['orb'=4,'gx'=2,'gyz'=4] {'gyz'}, use_global_device_ids=true, to_apply=%region_28.29 | all-reduce | flops 6 | bytes 48 | tf_op jit(solution)/shard_map/psum | solution.py:116
  147.4 4.9 %all-reduce.20 = (f32[3]{0:T(128)S(1)}, f32[3]{0:T(128)S(1)}) all-reduce(f32[3]{0:T(128)S(1)} %get-tuple-element.74, f32[3]{0:T(128)S(1)} %get-tuple-element.75), channel_id=1, replica_groups=mesh['orb'=4,'gx'=2,'gyz'=4] {'gx'}, use_global_device_ids=true, to_apply=%region_29.30 | all-reduce | flops 6 | bytes 48 | tf_op jit(solution)/shard_map/psum | solution.py:116
  154.1 1.9 collective-permute-start.17
  156.0 1.5 collective-permute-start.16
  157.7 4.3 %collective-permute-done.16 = f32[2,3,2,8,128]{4,3,2,1,0:T(8,128)S(1)} collective-permute-done((f32[2,3,2,8,128]{4,3,2,1,0:T(8,128)S(1)}, f32[2,3,2,8,128]{4,3,2,1,0:T(8,128)S(1)}, u32[]{:S(2)}, u32[]{:S(2)}) %collective-permute-start.16) | collective-permute-done | bytes 49184 | tf_op jit(solution)/shard_map/ppermute | solution.py:22
  162.1 3.2 collective-permute-start.19
  167.7 4.4 %collective-permute-done.18 = f32[2,3,20,2,128]{4,3,2,1,0:T(2,128)S(1)} collective-permute-done((f32[2,3,20,2,128]{4,3,2,1,0:T(2,128)S(1)}, f32[2,3,20,2,128]{4,3,2,1,0:T(2,128)S(1)}, u32[]{:S(2)}, u32[]{:S(2)}) %collective-permute-start.18) | collective-permute-done | bytes 122912 | tf_op jit(solution)/shard_map/ppermute | solution.py:22
  175.0 17.4 %all-reduce.11 = (f32[3]{0:T(128)S(1)}, f32[3]{0:T(128)S(1)}, f32[3]{0:T(128)S(1)}, f32[3]{0:T(128)S(1)}, f32[3]{0:T(128)S(1)}, /*index=5*/f32[3]{0:T(128)S(1)}, f32[3]{0:T(128)S(1)}) all-reduce(f32[3]{0:T(128)} %get-tuple-element.36, f32[3]{0:T(128)S(1)} %fusion.81, ...), channel_id=1, replica_groups=mesh['orb'=4,'gx'=2,'gyz'=4] {'gx','gyz'}, use_global_device_ids=true, to_apply=%region_35.36 | all-reduce | flops 21 | bytes 168 | tf_op jit(solution)/shard_map/psum | solution.py:124
  193.1 1.9 multiply_subtract_fusion.12
  197.0 2.9 collective-permute-start.21
  201.7 4.3 %collective-permute-done.20 = f32[2,3,2,8,128]{4,3,2,1,0:T(8,128)S(1)} collective-permute-done((f32[2,3,2,8,128]{4,3,2,1,0:T(8,128)S(1)}, f32[2,3,2,8,128]{4,3,2,1,0:T(8,128)S(1)}, u32[]{:S(2)}, u32[]{:S(2)}) %collective-permute-start.20) | collective-permute-done | bytes 49184 | tf_op jit(solution)/shard_map/ppermute | solution.py:22
  206.0 2.4 collective-permute-start.23
  210.9 4.4 %collective-permute-done.22 = f32[2,3,20,2,128]{4,3,2,1,0:T(2,128)S(1)} collective-permute-done((f32[2,3,20,2,128]{4,3,2,1,0:T(2,128)S(1)}, f32[2,3,20,2,128]{4,3,2,1,0:T(2,128)S(1)}, u32[]{:S(2)}, u32[]{:S(2)}) %collective-permute-start.22) | collective-permute-done | bytes 122912 | tf_op jit(solution)/shard_map/ppermute | solution.py:22
  217.2 8.9 %all-reduce.15 = (f32[3]{0:T(128)S(1)}, f32[3]{0:T(128)S(1)}) all-reduce(f32[3]{0:T(128)S(1)} %get-tuple-element.15, f32[3]{0:T(128)S(1)} %get-tuple-element.14), channel_id=1, replica_groups=mesh['orb'=4,'gx'=2,'gyz'=4] {'gyz'}, use_global_device_ids=true, to_apply=%region_48.49 | all-reduce | flops 6 | bytes 48 | tf_op jit(solution)/shard_map/psum | solution.py:116
  226.1 4.9 %all-reduce.19 = (f32[3]{0:T(128)S(1)}, f32[3]{0:T(128)S(1)}) all-reduce(f32[3]{0:T(128)S(1)} %get-tuple-element.72, f32[3]{0:T(128)S(1)} %get-tuple-element.73), channel_id=1, replica_groups=mesh['orb'=4,'gx'=2,'gyz'=4] {'gx'}, use_global_device_ids=true, to_apply=%region_49.50 | all-reduce | flops 6 | bytes 48 | tf_op jit(solution)/shard_map/psum | solution.py:116
  232.9 1.9 collective-permute-start.25
  234.8 1.3 collective-permute-start.24
  236.6 4.3 %collective-permute-done.24 = f32[2,3,2,8,128]{4,3,2,1,0:T(8,128)S(1)} collective-permute-done((f32[2,3,2,8,128]{4,3,2,1,0:T(8,128)S(1)}, f32[2,3,2,8,128]{4,3,2,1,0:T(8,128)S(1)}, u32[]{:S(2)}, u32[]{:S(2)}) %collective-permute-start.24) | collective-permute-done | bytes 49184 | tf_op jit(solution)/shard_map/ppermute | solution.py:22
  240.9 3.3 collective-permute-start.27
  245.6 1.9 collective-permute-done.27
  247.5 4.7 %collective-permute-done.26 = f32[2,3,20,2,128]{4,3,2,1,0:T(2,128)S(1)} collective-permute-done((f32[2,3,20,2,128]{4,3,2,1,0:T(2,128)S(1)}, f32[2,3,20,2,128]{4,3,2,1,0:T(2,128)S(1)}, u32[]{:S(2)}, u32[]{:S(2)}) %collective-permute-start.26) | collective-permute-done | bytes 122912 | tf_op jit(solution)/shard_map/ppermute | solution.py:22
  255.7 17.9 %all-reduce.10 = (f32[3]{0:T(128)}, f32[3]{0:T(128)}, f32[3]{0:T(128)}, f32[3]{0:T(128)}, f32[3]{0:T(128)}, /*index=5*/f32[3]{0:T(128)}, f32[3]{0:T(128)}) all-reduce(f32[3]{0:T(128)} %get-tuple-element.32, f32[3]{0:T(128)} %fusion.82, f32[3]{0:T(128)} %get-tuple-element.33, ...), channel_id=1, replica_groups=mesh['orb'=4,'gx'=2,'gyz'=4] {'gx','gyz'}, use_global_device_ids=true, to_apply=%region_55.56 | all-reduce | flops 21 | bytes 168 | tf_op jit(solution)/shard_map/psum | solution.py:124
  273.6 1.3 multiply_subtract_fusion.22
  275.0 2.2 multiply_subtract_fusion.6
  278.1 2.4 collective-permute-start.29
  282.2 4.3 %collective-permute-done.28 = f32[2,3,2,8,128]{4,3,2,1,0:T(8,128)S(1)} collective-permute-done((f32[2,3,2,8,128]{4,3,2,1,0:T(8,128)S(1)}, f32[2,3,2,8,128]{4,3,2,1,0:T(8,128)S(1)}, u32[]{:S(2)}, u32[]{:S(2)}) %collective-permute-start.28) | collective-permute-done | bytes 49184 | tf_op jit(solution)/shard_map/ppermute | solution.py:22
  286.5 2.8 collective-permute-start.31
  289.3 1.5 collective-permute-start.30
  291.8 4.4 %collective-permute-done.30 = f32[2,3,20,2,128]{4,3,2,1,0:T(2,128)S(1)} collective-permute-done((f32[2,3,20,2,128]{4,3,2,1,0:T(2,128)S(1)}, f32[2,3,20,2,128]{4,3,2,1,0:T(2,128)S(1)}, u32[]{:S(2)}, u32[]{:S(2)}) %collective-permute-start.30) | collective-permute-done | bytes 122912 | tf_op jit(solution)/shard_map/ppermute | solution.py:22
  298.6 9.1 %all-reduce.14 = (f32[3]{0:T(128)S(1)}, f32[3]{0:T(128)S(1)}) all-reduce(f32[3]{0:T(128)S(1)} %get-tuple-element.7, f32[3]{0:T(128)S(1)} %get-tuple-element.6), channel_id=1, replica_groups=mesh['orb'=4,'gx'=2,'gyz'=4] {'gyz'}, use_global_device_ids=true, to_apply=%region_68.69 | all-reduce | flops 6 | bytes 48 | tf_op jit(solution)/shard_map/psum | solution.py:116
  307.7 4.9 %all-reduce.18 = (f32[3]{0:T(128)S(1)}, f32[3]{0:T(128)S(1)}) all-reduce(f32[3]{0:T(128)S(1)} %get-tuple-element.70, f32[3]{0:T(128)S(1)} %get-tuple-element.71), channel_id=1, replica_groups=mesh['orb'=4,'gx'=2,'gyz'=4] {'gx'}, use_global_device_ids=true, to_apply=%region_69.70 | all-reduce | flops 6 | bytes 48 | tf_op jit(solution)/shard_map/psum | solution.py:116
  312.6 1.9 multiply_subtract_fusion.2
  316.5 1.9 collective-permute-start.33
  320.2 4.3 %collective-permute-done.32 = f32[2,3,2,8,128]{4,3,2,1,0:T(8,128)S(1)} collective-permute-done((f32[2,3,2,8,128]{4,3,2,1,0:T(8,128)S(1)}, f32[2,3,2,8,128]{4,3,2,1,0:T(8,128)S(1)}, u32[]{:S(2)}, u32[]{:S(2)}) %collective-permute-start.32) | collective-permute-done | bytes 49184 | tf_op jit(solution)/shard_map/ppermute | solution.py:22
  324.5 3.1 collective-permute-start.35
  330.1 4.4 %collective-permute-done.34 = f32[2,3,20,2,128]{4,3,2,1,0:T(2,128)S(1)} collective-permute-done((f32[2,3,20,2,128]{4,3,2,1,0:T(2,128)S(1)}, f32[2,3,20,2,128]{4,3,2,1,0:T(2,128)S(1)}, u32[]{:S(2)}, u32[]{:S(2)}) %collective-permute-start.34) | collective-permute-done | bytes 122912 | tf_op jit(solution)/shard_map/ppermute | solution.py:22
  337.3 17.2 %all-reduce.9 = (f32[3]{0:T(128)S(1)}, f32[3]{0:T(128)S(1)}, f32[3]{0:T(128)S(1)}) all-reduce(f32[3]{0:T(128)S(1)} %get-tuple-element.5, f32[3]{0:T(128)S(1)} %fusion.83, f32[3]{0:T(128)S(1)} %get-tuple-element.4), channel_id=1, replica_groups=mesh['orb'=4,'gx'=2,'gyz'=4] {'gx','gyz'}, use_global_device_ids=true, to_apply=%region_75.76 | all-reduce | flops 9 | bytes 72 | tf_op jit(solution)/shard_map/psum | solution.py:124
  355.8 2.1 maximum_subtract_fusion.10
  (212 shorter events, 63.0 us)
Async XLA Ops:
  0.6 16.7 %copy-start = (f32[16,8,128]{2,1,0:T(8,128)S(1)}, f32[16,8,128]{2,1,0:T(8,128)}, u32[]{:S(2)}) copy-start(f32[16,8,128]{2,1,0:T(8,128)} %param.3) | copy-start | bytes 196612
  1.5 6.6 %collective-permute-start.1 = (f32[2,3,2,8,128]{4,3,2,1,0:T(8,128)S(1)}, f32[2,3,2,8,128]{4,3,2,1,0:T(8,128)S(1)}, u32[]{:S(2)}, u32[]{:S(2)}) collective-permute-start(f32[2,3,2,8,128]{4,3,2,1,0:T(8,128)S(1)} %get-tuple-element.252), channel_id=1, source_target_pairs={{0,4},{1,5},{2,6},{3,7},{8,12},{9,13},{10,14},{11,15},{16,20},{17,... | collective-permute-start | bytes 147464 | tf_op jit(solution)/shard_map/ppermute | solution.py:21
  6.4 6.0 %collective-permute-start = (f32[2,3,2,8,128]{4,3,2,1,0:T(8,128)S(1)}, f32[2,3,2,8,128]{4,3,2,1,0:T(8,128)S(1)}, u32[]{:S(2)}, u32[]{:S(2)}) collective-permute-start(f32[2,3,2,8,128]{4,3,2,1,0:T(8,128)S(1)} %get-tuple-element.251), channel_id=1, source_target_pairs={{4,0},{5,1},{6,2},{7,3},{12,8},{13,9},{14,10},{15,11},{20,16},{21,... | collective-permute-start | bytes 147464 | tf_op jit(solution)/shard_map/ppermute | solution.py:22
  9.2 14.6 %copy-start.1 = (f32[2,3,16,8,128]{4,3,2,1,0:T(8,128)S(1)}, f32[2,3,16,8,128]{4,3,2,1,0:T(8,128)}, u32[]{:S(2)}) copy-start(f32[2,3,16,8,128]{4,3,2,1,0:T(8,128)} %param.2) | copy-start | bytes 1179652
  12.5 5.9 %collective-permute-start.3 = (f32[2,3,20,2,128]{4,3,2,1,0:T(2,128)S(1)}, f32[2,3,20,2,128]{4,3,2,1,0:T(2,128)S(1)}, u32[]{:S(2)}, u32[]{:S(2)}) collective-permute-start(f32[2,3,20,2,128]{4,3,2,1,0:T(2,128)S(1)} %get-tuple-element.166), channel_id=1, source_target_pairs={{0,1},{1,2},{2,3},{4,5},{5,6},{6,7},{8,9},{9,10},{10,11},{12,13},{... | collective-permute-start | bytes 368648 | tf_op jit(solution)/shard_map/ppermute | solution.py:21
  16.0 6.8 %collective-permute-start.2 = (f32[2,3,20,2,128]{4,3,2,1,0:T(2,128)S(1)}, f32[2,3,20,2,128]{4,3,2,1,0:T(2,128)S(1)}, u32[]{:S(2)}, u32[]{:S(2)}) collective-permute-start(f32[2,3,20,2,128]{4,3,2,1,0:T(2,128)S(1)} %get-tuple-element.167), channel_id=1, source_target_pairs={{1,0},{2,1},{3,2},{5,4},{6,5},{7,6},{9,8},{10,9},{11,10},{13,12},{... | collective-permute-start | bytes 368648 | tf_op jit(solution)/shard_map/ppermute | solution.py:22
  24.6 3.3 collective-permute-start.5
  26.2 6.0 %collective-permute-start.4 = (f32[2,3,2,8,128]{4,3,2,1,0:T(8,128)S(1)}, f32[2,3,2,8,128]{4,3,2,1,0:T(8,128)S(1)}, u32[]{:S(2)}, u32[]{:S(2)}) collective-permute-start(f32[2,3,2,8,128]{4,3,2,1,0:T(8,128)S(1)} %get-tuple-element.247), channel_id=1, source_target_pairs={{4,0},{5,1},{6,2},{7,3},{12,8},{13,9},{14,10},{15,11},{20,16},{21,... | collective-permute-start | bytes 147464 | tf_op jit(solution)/shard_map/ppermute | solution.py:22
  32.2 5.9 %collective-permute-start.7 = (f32[2,3,20,2,128]{4,3,2,1,0:T(2,128)S(1)}, f32[2,3,20,2,128]{4,3,2,1,0:T(2,128)S(1)}, u32[]{:S(2)}, u32[]{:S(2)}) collective-permute-start(f32[2,3,20,2,128]{4,3,2,1,0:T(2,128)S(1)} %get-tuple-element.164), channel_id=1, source_target_pairs={{0,1},{1,2},{2,3},{4,5},{5,6},{6,7},{8,9},{9,10},{10,11},{12,13},{... | collective-permute-start | bytes 368648 | tf_op jit(solution)/shard_map/ppermute | solution.py:21
  35.7 6.8 %collective-permute-start.6 = (f32[2,3,20,2,128]{4,3,2,1,0:T(2,128)S(1)}, f32[2,3,20,2,128]{4,3,2,1,0:T(2,128)S(1)}, u32[]{:S(2)}, u32[]{:S(2)}) collective-permute-start(f32[2,3,20,2,128]{4,3,2,1,0:T(2,128)S(1)} %get-tuple-element.165), channel_id=1, source_target_pairs={{1,0},{2,1},{3,2},{5,4},{6,5},{7,6},{9,8},{10,9},{11,10},{13,12},{... | collective-permute-start | bytes 368648 | tf_op jit(solution)/shard_map/ppermute | solution.py:22
  78.1 5.2 %collective-permute-start.9 = (f32[2,3,2,8,128]{4,3,2,1,0:T(8,128)S(1)}, f32[2,3,2,8,128]{4,3,2,1,0:T(8,128)S(1)}, u32[]{:S(2)}, u32[]{:S(2)}) collective-permute-start(f32[2,3,2,8,128]{4,3,2,1,0:T(8,128)S(1)} %get-tuple-element.240), channel_id=1, source_target_pairs={{0,4},{1,5},{2,6},{3,7},{8,12},{9,13},{10,14},{11,15},{16,20},{17,... | collective-permute-start | bytes 147464 | tf_op jit(solution)/shard_map/ppermute | solution.py:21
  81.5 6.0 %collective-permute-start.8 = (f32[2,3,2,8,128]{4,3,2,1,0:T(8,128)S(1)}, f32[2,3,2,8,128]{4,3,2,1,0:T(8,128)S(1)}, u32[]{:S(2)}, u32[]{:S(2)}) collective-permute-start(f32[2,3,2,8,128]{4,3,2,1,0:T(8,128)S(1)} %get-tuple-element.241), channel_id=1, source_target_pairs={{4,0},{5,1},{6,2},{7,3},{12,8},{13,9},{14,10},{15,11},{20,16},{21,... | collective-permute-start | bytes 147464 | tf_op jit(solution)/shard_map/ppermute | solution.py:22
  87.6 4.5 %collective-permute-start.11 = (f32[2,3,20,2,128]{4,3,2,1,0:T(2,128)S(1)}, f32[2,3,20,2,128]{4,3,2,1,0:T(2,128)S(1)}, u32[]{:S(2)}, u32[]{:S(2)}) collective-permute-start(f32[2,3,20,2,128]{4,3,2,1,0:T(2,128)S(1)} %get-tuple-element.162), channel_id=1, source_target_pairs={{0,1},{1,2},{2,3},{4,5},{5,6},{6,7},{8,9},{9,10},{10,11},{12,13},{... | collective-permute-start | bytes 368648 | tf_op jit(solution)/shard_map/ppermute | solution.py:21
  89.6 6.8 %collective-permute-start.10 = (f32[2,3,20,2,128]{4,3,2,1,0:T(2,128)S(1)}, f32[2,3,20,2,128]{4,3,2,1,0:T(2,128)S(1)}, u32[]{:S(2)}, u32[]{:S(2)}) collective-permute-start(f32[2,3,20,2,128]{4,3,2,1,0:T(2,128)S(1)} %get-tuple-element.163), channel_id=1, source_target_pairs={{1,0},{2,1},{3,2},{5,4},{6,5},{7,6},{9,8},{10,9},{11,10},{13,12},{... | collective-permute-start | bytes 368648 | tf_op jit(solution)/shard_map/ppermute | solution.py:22
  116.2 36.1 %copy-start.34 = (f32[3]{0:T(128)}, f32[3]{0:T(128)S(1)}, u32[]{:S(2)}) copy-start(f32[3]{0:T(128)S(1)} %get-tuple-element.115) | copy-start | bytes 40
  116.2 36.1 %copy-start.35 = (f32[3]{0:T(128)}, f32[3]{0:T(128)S(1)}, u32[]{:S(2)}) copy-start(f32[3]{0:T(128)S(1)} %get-tuple-element.116) | copy-start | bytes 40
  118.2 5.1 %collective-permute-start.13 = (f32[2,3,2,8,128]{4,3,2,1,0:T(8,128)S(1)}, f32[2,3,2,8,128]{4,3,2,1,0:T(8,128)S(1)}, u32[]{:S(2)}, u32[]{:S(2)}) collective-permute-start(f32[2,3,2,8,128]{4,3,2,1,0:T(8,128)S(1)} %get-tuple-element.234), channel_id=1, source_target_pairs={{0,4},{1,5},{2,6},{3,7},{8,12},{9,13},{10,14},{11,15},{16,20},{17,... | collective-permute-start | bytes 147464 | tf_op jit(solution)/shard_map/ppermute | solution.py:21
  121.6 6.0 %collective-permute-start.12 = (f32[2,3,2,8,128]{4,3,2,1,0:T(8,128)S(1)}, f32[2,3,2,8,128]{4,3,2,1,0:T(8,128)S(1)}, u32[]{:S(2)}, u32[]{:S(2)}) collective-permute-start(f32[2,3,2,8,128]{4,3,2,1,0:T(8,128)S(1)} %get-tuple-element.235), channel_id=1, source_target_pairs={{4,0},{5,1},{6,2},{7,3},{12,8},{13,9},{14,10},{15,11},{20,16},{21,... | collective-permute-start | bytes 147464 | tf_op jit(solution)/shard_map/ppermute | solution.py:22
  127.7 4.3 %collective-permute-start.15 = (f32[2,3,20,2,128]{4,3,2,1,0:T(2,128)S(1)}, f32[2,3,20,2,128]{4,3,2,1,0:T(2,128)S(1)}, u32[]{:S(2)}, u32[]{:S(2)}) collective-permute-start(f32[2,3,20,2,128]{4,3,2,1,0:T(2,128)S(1)} %get-tuple-element.160), channel_id=1, source_target_pairs={{0,1},{1,2},{2,3},{4,5},{5,6},{6,7},{8,9},{9,10},{10,11},{12,13},{... | collective-permute-start | bytes 368648 | tf_op jit(solution)/shard_map/ppermute | solution.py:21
  129.5 6.8 %collective-permute-start.14 = (f32[2,3,20,2,128]{4,3,2,1,0:T(2,128)S(1)}, f32[2,3,20,2,128]{4,3,2,1,0:T(2,128)S(1)}, u32[]{:S(2)}, u32[]{:S(2)}) collective-permute-start(f32[2,3,20,2,128]{4,3,2,1,0:T(2,128)S(1)} %get-tuple-element.161), channel_id=1, source_target_pairs={{1,0},{2,1},{3,2},{5,4},{6,5},{7,6},{9,8},{10,9},{11,10},{13,12},{... | collective-permute-start | bytes 368648 | tf_op jit(solution)/shard_map/ppermute | solution.py:22
  154.1 3.6 %collective-permute-start.17 = (f32[2,3,2,8,128]{4,3,2,1,0:T(8,128)S(1)}, f32[2,3,2,8,128]{4,3,2,1,0:T(8,128)S(1)}, u32[]{:S(2)}, u32[]{:S(2)}) collective-permute-start(f32[2,3,2,8,128]{4,3,2,1,0:T(8,128)S(1)} %get-tuple-element.230), channel_id=1, source_target_pairs={{0,4},{1,5},{2,6},{3,7},{8,12},{9,13},{10,14},{11,15},{16,20},{17,... | collective-permute-start | bytes 147464 | tf_op jit(solution)/shard_map/ppermute | solution.py:21
  156.0 6.0 %collective-permute-start.16 = (f32[2,3,2,8,128]{4,3,2,1,0:T(8,128)S(1)}, f32[2,3,2,8,128]{4,3,2,1,0:T(8,128)S(1)}, u32[]{:S(2)}, u32[]{:S(2)}) collective-permute-start(f32[2,3,2,8,128]{4,3,2,1,0:T(8,128)S(1)} %get-tuple-element.231), channel_id=1, source_target_pairs={{4,0},{5,1},{6,2},{7,3},{12,8},{13,9},{14,10},{15,11},{20,16},{21,... | collective-permute-start | bytes 147464 | tf_op jit(solution)/shard_map/ppermute | solution.py:22
  162.1 5.6 %collective-permute-start.19 = (f32[2,3,20,2,128]{4,3,2,1,0:T(2,128)S(1)}, f32[2,3,20,2,128]{4,3,2,1,0:T(2,128)S(1)}, u32[]{:S(2)}, u32[]{:S(2)}) collective-permute-start(f32[2,3,20,2,128]{4,3,2,1,0:T(2,128)S(1)} %get-tuple-element.158), channel_id=1, source_target_pairs={{0,1},{1,2},{2,3},{4,5},{5,6},{6,7},{8,9},{9,10},{10,11},{12,13},{... | collective-permute-start | bytes 368648 | tf_op jit(solution)/shard_map/ppermute | solution.py:21
  165.2 6.8 %collective-permute-start.18 = (f32[2,3,20,2,128]{4,3,2,1,0:T(2,128)S(1)}, f32[2,3,20,2,128]{4,3,2,1,0:T(2,128)S(1)}, u32[]{:S(2)}, u32[]{:S(2)}) collective-permute-start(f32[2,3,20,2,128]{4,3,2,1,0:T(2,128)S(1)} %get-tuple-element.159), channel_id=1, source_target_pairs={{1,0},{2,1},{3,2},{5,4},{6,5},{7,6},{9,8},{10,9},{11,10},{13,12},{... | collective-permute-start | bytes 368648 | tf_op jit(solution)/shard_map/ppermute | solution.py:22
  197.0 4.7 %collective-permute-start.21 = (f32[2,3,2,8,128]{4,3,2,1,0:T(8,128)S(1)}, f32[2,3,2,8,128]{4,3,2,1,0:T(8,128)S(1)}, u32[]{:S(2)}, u32[]{:S(2)}) collective-permute-start(f32[2,3,2,8,128]{4,3,2,1,0:T(8,128)S(1)} %get-tuple-element.224), channel_id=1, source_target_pairs={{0,4},{1,5},{2,6},{3,7},{8,12},{9,13},{10,14},{11,15},{16,20},{17,... | collective-permute-start | bytes 147464 | tf_op jit(solution)/shard_map/ppermute | solution.py:21
  199.9 6.0 %collective-permute-start.20 = (f32[2,3,2,8,128]{4,3,2,1,0:T(8,128)S(1)}, f32[2,3,2,8,128]{4,3,2,1,0:T(8,128)S(1)}, u32[]{:S(2)}, u32[]{:S(2)}) collective-permute-start(f32[2,3,2,8,128]{4,3,2,1,0:T(8,128)S(1)} %get-tuple-element.225), channel_id=1, source_target_pairs={{4,0},{5,1},{6,2},{7,3},{12,8},{13,9},{14,10},{15,11},{20,16},{21,... | collective-permute-start | bytes 147464 | tf_op jit(solution)/shard_map/ppermute | solution.py:22
  206.0 4.9 %collective-permute-start.23 = (f32[2,3,20,2,128]{4,3,2,1,0:T(2,128)S(1)}, f32[2,3,20,2,128]{4,3,2,1,0:T(2,128)S(1)}, u32[]{:S(2)}, u32[]{:S(2)}) collective-permute-start(f32[2,3,20,2,128]{4,3,2,1,0:T(2,128)S(1)} %get-tuple-element.156), channel_id=1, source_target_pairs={{0,1},{1,2},{2,3},{4,5},{5,6},{6,7},{8,9},{9,10},{10,11},{12,13},{... | collective-permute-start | bytes 368648 | tf_op jit(solution)/shard_map/ppermute | solution.py:21
  208.5 6.8 %collective-permute-start.22 = (f32[2,3,20,2,128]{4,3,2,1,0:T(2,128)S(1)}, f32[2,3,20,2,128]{4,3,2,1,0:T(2,128)S(1)}, u32[]{:S(2)}, u32[]{:S(2)}) collective-permute-start(f32[2,3,20,2,128]{4,3,2,1,0:T(2,128)S(1)} %get-tuple-element.157), channel_id=1, source_target_pairs={{1,0},{2,1},{3,2},{5,4},{6,5},{7,6},{9,8},{10,9},{11,10},{13,12},{... | collective-permute-start | bytes 368648 | tf_op jit(solution)/shard_map/ppermute | solution.py:22
  231.9 0.8 copy-start.10
  232.9 3.6 %collective-permute-start.25 = (f32[2,3,2,8,128]{4,3,2,1,0:T(8,128)S(1)}, f32[2,3,2,8,128]{4,3,2,1,0:T(8,128)S(1)}, u32[]{:S(2)}, u32[]{:S(2)}) collective-permute-start(f32[2,3,2,8,128]{4,3,2,1,0:T(8,128)S(1)} %get-tuple-element.220), channel_id=1, source_target_pairs={{0,4},{1,5},{2,6},{3,7},{8,12},{9,13},{10,14},{11,15},{16,20},{17,... | collective-permute-start | bytes 147464 | tf_op jit(solution)/shard_map/ppermute | solution.py:21
  234.8 6.0 %collective-permute-start.24 = (f32[2,3,2,8,128]{4,3,2,1,0:T(8,128)S(1)}, f32[2,3,2,8,128]{4,3,2,1,0:T(8,128)S(1)}, u32[]{:S(2)}, u32[]{:S(2)}) collective-permute-start(f32[2,3,2,8,128]{4,3,2,1,0:T(8,128)S(1)} %get-tuple-element.221), channel_id=1, source_target_pairs={{4,0},{5,1},{6,2},{7,3},{12,8},{13,9},{14,10},{15,11},{20,16},{21,... | collective-permute-start | bytes 147464 | tf_op jit(solution)/shard_map/ppermute | solution.py:22
  240.9 6.6 %collective-permute-start.27 = (f32[2,3,20,2,128]{4,3,2,1,0:T(2,128)S(1)}, f32[2,3,20,2,128]{4,3,2,1,0:T(2,128)S(1)}, u32[]{:S(2)}, u32[]{:S(2)}) collective-permute-start(f32[2,3,20,2,128]{4,3,2,1,0:T(2,128)S(1)} %get-tuple-element.154), channel_id=1, source_target_pairs={{0,1},{1,2},{2,3},{4,5},{5,6},{6,7},{8,9},{9,10},{10,11},{12,13},{... | collective-permute-start | bytes 368648 | tf_op jit(solution)/shard_map/ppermute | solution.py:21
  244.2 7.9 %collective-permute-start.26 = (f32[2,3,20,2,128]{4,3,2,1,0:T(2,128)S(1)}, f32[2,3,20,2,128]{4,3,2,1,0:T(2,128)S(1)}, u32[]{:S(2)}, u32[]{:S(2)}) collective-permute-start(f32[2,3,20,2,128]{4,3,2,1,0:T(2,128)S(1)} %get-tuple-element.155), channel_id=1, source_target_pairs={{1,0},{2,1},{3,2},{5,4},{6,5},{7,6},{9,8},{10,9},{11,10},{13,12},{... | collective-permute-start | bytes 368648 | tf_op jit(solution)/shard_map/ppermute | solution.py:22
  254.0 1.0 copy-start.7
  254.0 20.9 %copy-start.6 = (f32[1,3,16,8,128]{4,3,2,1,0:T(8,128)}, f32[1,3,16,8,128]{4,3,2,1,0:T(8,128)S(1)}, u32[]{:S(2)}) copy-start(f32[1,3,16,8,128]{4,3,2,1,0:T(8,128)S(1)} %get-tuple-element.216) | copy-start | bytes 589828
  273.6 3.5 copy-start.15
  273.6 3.5 copy-start.17
  278.1 4.1 %collective-permute-start.29 = (f32[2,3,2,8,128]{4,3,2,1,0:T(8,128)S(1)}, f32[2,3,2,8,128]{4,3,2,1,0:T(8,128)S(1)}, u32[]{:S(2)}, u32[]{:S(2)}) collective-permute-start(f32[2,3,2,8,128]{4,3,2,1,0:T(8,128)S(1)} %get-tuple-element.214), channel_id=1, source_target_pairs={{0,4},{1,5},{2,6},{3,7},{8,12},{9,13},{10,14},{11,15},{16,20},{17,... | collective-permute-start | bytes 147464 | tf_op jit(solution)/shard_map/ppermute | solution.py:21
  280.5 6.0 %collective-permute-start.28 = (f32[2,3,2,8,128]{4,3,2,1,0:T(8,128)S(1)}, f32[2,3,2,8,128]{4,3,2,1,0:T(8,128)S(1)}, u32[]{:S(2)}, u32[]{:S(2)}) collective-permute-start(f32[2,3,2,8,128]{4,3,2,1,0:T(8,128)S(1)} %get-tuple-element.215), channel_id=1, source_target_pairs={{4,0},{5,1},{6,2},{7,3},{12,8},{13,9},{14,10},{15,11},{20,16},{21,... | collective-permute-start | bytes 147464 | tf_op jit(solution)/shard_map/ppermute | solution.py:22
  286.5 5.2 %collective-permute-start.31 = (f32[2,3,20,2,128]{4,3,2,1,0:T(2,128)S(1)}, f32[2,3,20,2,128]{4,3,2,1,0:T(2,128)S(1)}, u32[]{:S(2)}, u32[]{:S(2)}) collective-permute-start(f32[2,3,20,2,128]{4,3,2,1,0:T(2,128)S(1)} %get-tuple-element.152), channel_id=1, source_target_pairs={{0,1},{1,2},{2,3},{4,5},{5,6},{6,7},{8,9},{9,10},{10,11},{12,13},{... | collective-permute-start | bytes 368648 | tf_op jit(solution)/shard_map/ppermute | solution.py:21
  289.3 6.8 %collective-permute-start.30 = (f32[2,3,20,2,128]{4,3,2,1,0:T(2,128)S(1)}, f32[2,3,20,2,128]{4,3,2,1,0:T(2,128)S(1)}, u32[]{:S(2)}, u32[]{:S(2)}) collective-permute-start(f32[2,3,20,2,128]{4,3,2,1,0:T(2,128)S(1)} %get-tuple-element.153), channel_id=1, source_target_pairs={{1,0},{2,1},{3,2},{5,4},{6,5},{7,6},{9,8},{10,9},{11,10},{13,12},{... | collective-permute-start | bytes 368648 | tf_op jit(solution)/shard_map/ppermute | solution.py:22
  297.9 14.7 %copy-start.36 = (f32[3]{0:T(128)S(1)}, f32[3]{0:T(128)}, u32[]{:S(2)}) copy-start(f32[3]{0:T(128)} %get-tuple-element.91) | copy-start | bytes 40
  297.9 14.7 %copy-start.37 = (f32[3]{0:T(128)S(1)}, f32[3]{0:T(128)}, u32[]{:S(2)}) copy-start(f32[3]{0:T(128)} %get-tuple-element.92) | copy-start | bytes 40
  314.6 0.8 copy-start.19
  316.5 3.6 %collective-permute-start.33 = (f32[2,3,2,8,128]{4,3,2,1,0:T(8,128)S(1)}, f32[2,3,2,8,128]{4,3,2,1,0:T(8,128)S(1)}, u32[]{:S(2)}, u32[]{:S(2)}) collective-permute-start(f32[2,3,2,8,128]{4,3,2,1,0:T(8,128)S(1)} %get-tuple-element.210), channel_id=1, source_target_pairs={{0,4},{1,5},{2,6},{3,7},{8,12},{9,13},{10,14},{11,15},{16,20},{17,... | collective-permute-start | bytes 147464 | tf_op jit(solution)/shard_map/ppermute | solution.py:21
  318.4 6.0 %collective-permute-start.32 = (f32[2,3,2,8,128]{4,3,2,1,0:T(8,128)S(1)}, f32[2,3,2,8,128]{4,3,2,1,0:T(8,128)S(1)}, u32[]{:S(2)}, u32[]{:S(2)}) collective-permute-start(f32[2,3,2,8,128]{4,3,2,1,0:T(8,128)S(1)} %get-tuple-element.211), channel_id=1, source_target_pairs={{4,0},{5,1},{6,2},{7,3},{12,8},{13,9},{14,10},{15,11},{20,16},{21,... | collective-permute-start | bytes 147464 | tf_op jit(solution)/shard_map/ppermute | solution.py:22
  324.5 5.6 %collective-permute-start.35 = (f32[2,3,20,2,128]{4,3,2,1,0:T(2,128)S(1)}, f32[2,3,20,2,128]{4,3,2,1,0:T(2,128)S(1)}, u32[]{:S(2)}, u32[]{:S(2)}) collective-permute-start(f32[2,3,20,2,128]{4,3,2,1,0:T(2,128)S(1)} %get-tuple-element.150), channel_id=1, source_target_pairs={{0,1},{1,2},{2,3},{4,5},{5,6},{6,7},{8,9},{9,10},{10,11},{12,13},{... | collective-permute-start | bytes 368648 | tf_op jit(solution)/shard_map/ppermute | solution.py:21
  327.6 6.8 %collective-permute-start.34 = (f32[2,3,20,2,128]{4,3,2,1,0:T(2,128)S(1)}, f32[2,3,20,2,128]{4,3,2,1,0:T(2,128)S(1)}, u32[]{:S(2)}, u32[]{:S(2)}) collective-permute-start(f32[2,3,20,2,128]{4,3,2,1,0:T(2,128)S(1)} %get-tuple-element.151), channel_id=1, source_target_pairs={{1,0},{2,1},{3,2},{5,4},{6,5},{7,6},{9,8},{10,9},{11,10},{13,12},{... | collective-permute-start | bytes 368648 | tf_op jit(solution)/shard_map/ppermute | solution.py:22
  336.1 19.4 %copy-start.5 = (f32[1,3,16,8,128]{4,3,2,1,0:T(8,128)S(1)}, f32[1,3,16,8,128]{4,3,2,1,0:T(8,128)}, u32[]{:S(2)}) copy-start(f32[1,3,16,8,128]{4,3,2,1,0:T(8,128)} %copy-done.4) | copy-start | bytes 589828
  355.6 2.3 copy-start.2
  355.6 2.3 copy-start.20
  355.6 2.3 copy-start.21
  355.6 2.3 copy-start.22
  355.6 2.3 copy-start.23
  355.7 2.3 copy-start.24
  355.7 2.3 copy-start.25
  355.7 2.3 copy-start.26
  355.7 2.3 copy-start.27
  355.7 2.3 copy-start.28
  355.7 2.3 copy-start.29
  355.7 2.3 copy-start.30
  355.7 2.3 copy-start.31
  355.7 2.3 copy-start.32
  355.7 2.3 copy-start.33
  (10 other events, 7.0 us)
